TPU v7x, 32 devices: a whole 2x2x4 slice. The times are simulated.
32 devices in a mesh: strip: 32 (over z, y, x, core).
Axes of the slice: x: 2, y: 2, z: 4, core: 2. Of those that a mesh axis runs over, the one named last changes fastest.
Arguments:
- state: float32 [4096, 4096], P('strip'), may hold values from -6 to 6
- noise: float32 [4096, 4096], P('strip'), may hold values from -6 to 6
- step: float32 [1], replicated, may hold values from 0.3 to 0.7
- field_scale: float32 [1], replicated, may hold values from 0.6 to 1.2
- wave_scale: float32 [1], replicated, may hold values from 4 to 8
- source: float32 [2048, 2048], P('strip'), may hold values from -6 to 6
- obs_cells: int32 [2048], replicated, may hold values from 0 to 4194303
- obs_values: float32 [2048], replicated, may hold values from -3 to 3
Outputs:
- log_perm: float32 [2048, 2048], P('strip')
- pressure: float32 [2048, 2048], P('strip')
- loglik: float32 [], replicated
Inputs may be any that keep to these rules, and one draw needn't show every extreme that they name: `obs_cells`: each entry is row * 2048 + column of an observed cell of the field grid.
All inputs are finite; a program needn't handle non-finite values.
Results may differ from a plain program's by a relative error of at most 0.00011.
Values sent between devices are 32-bit elements; how exact they have to be, the bound alone decides.
No kernel may reach another device: no remote copies, remote signals or barrier semaphores. Data moves between devices by JAX's collectives and lax.ppermute only.
A program may use at most 64 MiB of HBM per device.

v0:
```python
import math

import jax
import jax.numpy as jnp
from jax import lax
from jax.sharding import PartitionSpec as P

ITERS = 4


precise = lax.Precision.HIGHEST


def padded(block, sides, width):
    for axis, dim in sides:
        count = lax.axis_size(axis)
        forward = [(i, i + 1) for i in range(count - 1)]
        backward = [(target, source) for source, target in forward]
        low = lax.ppermute(
            lax.slice_in_dim(block, block.shape[dim] - width, None, axis=dim), axis, forward
        )
        high = lax.ppermute(lax.slice_in_dim(block, 0, width, axis=dim), axis, backward)
        block = jnp.concatenate([low, block, high], axis=dim)
    return block


def split_length(length):
    second = min(128, length)
    return (length // second, second)


def phase_table(height, breadth, modulus, orient):
    product = (
        lax.broadcasted_iota(jnp.int32, (height, breadth), 0)
        * lax.broadcasted_iota(jnp.int32, (height, breadth), 1)
        % modulus
    )
    angles = product.astype(jnp.float32) * (orient * 2.0 * math.pi / modulus)
    return (jnp.cos(angles), jnp.sin(angles))


def true_freq(index, factor, second):
    return index // second + factor * (index % second)


def forward_permuted(real_part, imag_part, orient):
    length = real_part.shape[-1]
    factor, second = split_length(length)
    leading = real_part.shape[:-1]
    inner_cos, inner_sin = phase_table(factor, factor, factor, orient)
    shaped = real_part.reshape(leading + (factor, second))
    section_real = jnp.einsum("kn,...na->...ka", inner_cos, shaped, precision=precise)
    section_imag = jnp.einsum("kn,...na->...ka", inner_sin, shaped, precision=precise)
    if imag_part is not None:
        shaped_imag = imag_part.reshape(leading + (factor, second))
        section_real = section_real - jnp.einsum(
            "kn,...na->...ka", inner_sin, shaped_imag, precision=precise
        )
        section_imag = section_imag + jnp.einsum(
            "kn,...na->...ka", inner_cos, shaped_imag, precision=precise
        )
    twist_cos, twist_sin = phase_table(factor, second, length, orient)
    turned_real = section_real * twist_cos - section_imag * twist_sin
    turned_imag = section_real * twist_sin + section_imag * twist_cos
    outer_cos, outer_sin = phase_table(second, second, second, orient)
    result_real = jnp.einsum(
        "ja,...ka->...kj", outer_cos, turned_real, precision=precise
    ) - jnp.einsum("ja,...ka->...kj", outer_sin, turned_imag, precision=precise)
    result_imag = jnp.einsum(
        "ja,...ka->...kj", outer_sin, turned_real, precision=precise
    ) + jnp.einsum("ja,...ka->...kj", outer_cos, turned_imag, precision=precise)
    return (result_real.reshape(leading + (length,)), result_imag.reshape(leading + (length,)))


def inverse_natural(real_part, imag_part, orient, keep, real_only=False):
    length = real_part.shape[-1]
    factor, second = split_length(length)
    leading = real_part.shape[:-1]
    shaped_real = real_part.reshape(leading + (factor, second))
    shaped_imag = imag_part.reshape(leading + (factor, second))
    inner_cos, inner_sin = phase_table(second, second, second, orient)
    section_real = jnp.einsum(
        "ak,...jk->...ja", inner_cos, shaped_real, precision=precise
    ) - jnp.einsum("ak,...jk->...ja", inner_sin, shaped_imag, precision=precise)
    section_imag = jnp.einsum(
        "ak,...jk->...ja", inner_sin, shaped_real, precision=precise
    ) + jnp.einsum("ak,...jk->...ja", inner_cos, shaped_imag, precision=precise)
    twist_cos, twist_sin = phase_table(factor, second, length, orient)
    turned_real = section_real * twist_cos - section_imag * twist_sin
    turned_imag = section_real * twist_sin + section_imag * twist_cos
    outer_cos, outer_sin = phase_table(keep // second, factor, factor, orient)
    result_real = jnp.einsum(
        "bj,...ja->...ba", outer_cos, turned_real, precision=precise
    ) - jnp.einsum("bj,...ja->...ba", outer_sin, turned_imag, precision=precise)
    result_real = result_real.reshape(leading + (keep,))
    if real_only:
        return (result_real, None)
    result_imag = jnp.einsum(
        "bj,...ja->...ba", outer_sin, turned_real, precision=precise
    ) + jnp.einsum("bj,...ja->...ba", outer_cos, turned_imag, precision=precise)
    return (result_real, result_imag.reshape(leading + (keep,)))


def amplitude(row_freq, col_freq, length, scale, wave):
    row_wave = jnp.minimum(row_freq, length - row_freq).astype(jnp.float32)
    col_wave = jnp.minimum(col_freq, length - col_freq).astype(jnp.float32)
    shape_term = 1.0 / (1.0 + (row_wave * row_wave + col_wave * col_wave) / (wave * wave))
    return scale * length / (wave * math.sqrt(math.pi)) * shape_term


def body(state, noise, step, field_scale, wave_scale, source, obs_cells, obs_values):
    parts = lax.axis_size("strip")
    position = lax.axis_index("strip")
    rows_here, length = state.shape
    half = length // 2
    factor, second = split_length(length)
    field_rows = source.shape[0]
    rate = step[0]
    sigma = field_scale[0]
    wave = wave_scale[0]
    mixed = jnp.sqrt(1.0 - rate * rate) * state + rate * noise
    row_freq = true_freq(lax.broadcasted_iota(jnp.int32, (1, length), 1), factor, second)
    width = length // parts
    freq_real, freq_imag = forward_permuted(mixed, None, -1.0)
    send_real = freq_real.reshape(rows_here, parts, width).transpose(1, 2, 0)
    send_imag = freq_imag.reshape(rows_here, parts, width).transpose(1, 2, 0)
    column_real, column_imag = (
        lax.all_to_all(send_real, "strip", split_axis=0, concat_axis=2, tiled=True),
        lax.all_to_all(send_imag, "strip", split_axis=0, concat_axis=2, tiled=True),
    )
    column_real = column_real.reshape(width, length)
    column_imag = column_imag.reshape(width, length)
    spec_real, spec_imag = forward_permuted(column_real, column_imag, -1.0)
    slot = position * width + lax.broadcasted_iota(jnp.int32, (width, 1), 0)
    col_freq = true_freq(slot, factor, second)
    scaled = amplitude(row_freq, col_freq, length, sigma, wave)
    field_real, field_imag = inverse_natural(scaled * spec_real, scaled * spec_imag, 1.0, half)
    back_real, back_imag = (
        lax.all_to_all(
            field_real.reshape(width, parts, field_rows),
            "strip",
            split_axis=1,
            concat_axis=0,
            tiled=True,
        ),
        lax.all_to_all(
            field_imag.reshape(width, parts, field_rows),
            "strip",
            split_axis=1,
            concat_axis=0,
            tiled=True,
        ),
    )
    lower_real = back_real.reshape(length, field_rows).T
    lower_imag = back_imag.reshape(length, field_rows).T
    log_perm = inverse_natural(lower_real, lower_imag, 1.0, half, True)[0] / (length * length)
    kappa = jnp.exp(log_perm)
    rimmed = padded(kappa, (("strip", 0),), 1)
    sided = jnp.pad(kappa, ((0, 0), (1, 1)))
    north = 0.5 * (kappa + rimmed[:-2])
    south = 0.5 * (kappa + rimmed[2:])
    west = 0.5 * (kappa + sided[:, :-2])
    east = 0.5 * (kappa + sided[:, 2:])
    diagonal = north + south + west + east
    pressure = jnp.zeros_like(source)
    residual = source
    direction = jnp.zeros_like(source)
    along = jnp.zeros_like(source)
    gamma_prior = jnp.float32(1.0)
    alpha_prior = jnp.float32(1.0)
    for iteration in range(ITERS):
        precond = residual / diagonal
        beside_all = padded(precond, (("strip", 0),), 1)
        beside = jnp.pad(precond, ((0, 0), (1, 1)))
        image = (
            diagonal * precond
            - north * beside_all[:-2]
            - south * beside_all[2:]
            - west * beside[:, :-2]
            - east * beside[:, 2:]
        )
        gamma, delta = lax.psum((jnp.sum(residual * precond), jnp.sum(precond * image)), "strip")
        if iteration == 0:
            alpha = gamma / delta
            direction = precond
            along = image
        else:
            ratio = gamma / gamma_prior
            alpha = gamma / (delta - ratio * gamma / alpha_prior)
            direction = precond + ratio * direction
            along = image + ratio * along
        pressure = pressure + alpha * direction
        residual = residual - alpha * along
        gamma_prior = gamma
        alpha_prior = alpha
    columns = pressure.shape[1]
    cell_row = obs_cells // columns
    cell_col = obs_cells % columns
    local_row = cell_row - position * field_rows
    inside = (local_row >= 0) & (local_row < field_rows)
    picked = pressure[jnp.clip(local_row, 0, field_rows - 1), cell_col]
    differ = jnp.where(inside, picked - obs_values, 0.0)
    total = lax.psum(jnp.sum(differ * differ), "strip")
    loglik = -(2.0 / obs_cells.shape[0]) * total
    return (log_perm, pressure, loglik)


def solution(mesh):
    placed = (P("strip", None), P("strip", None), P(), P(), P(), P("strip", None), P(), P())
    return jax.shard_map(
        body,
        mesh=mesh,
        in_specs=placed,
        out_specs=(P("strip", None), P("strip", None), P()),
        check_vma=False,
    )
```

profile of v0, /device:TPU:0, one launch (start us, length us, event | category | flops | bytes accessed | tf_op | source)
XLA Modules:
  0.0 528.5 jit_solution(12919456128651827685)
XLA Ops:
  8.6 3.6 fusion.22
  12.2 5.2 subtract_bitcast_fusion
  17.5 7.5 %all-to-all-start = ((f32[32,128,128]{1,2,0:T(8,128)}), f32[32,128,128]{1,2,0:T(8,128)}, u32[]{:S(2)}, u32[]{:S(2)}) async-start(f32[32,128,128]{1,2,0:T(8,128)} %subtract_bitcast_fusion), calls=%async_computation | async-start | bytes 4194304 | tf_op jit(solution)/shard_map/all_to_all | solution.py:128
  24.9 5.1 fusion.20
  30.1 4.9 add_bitcast_fusion
  35.0 38.6 %all-to-all-done = f32[32,128,128]{1,2,0:T(8,128)} async-done(((f32[32,128,128]{1,2,0:T(8,128)}), f32[32,128,128]{1,2,0:T(8,128)}, u32[]{:S(2)}, u32[]{:S(2)}) %all-to-all-start) | async-done | bytes 2097184 | tf_op jit(solution)/shard_map/all_to_all | solution.py:128
  73.7 4.2 all-to-all-start.1
  85.1 3.3 fusion.168
  88.4 38.2 %all-to-all-done.1 = f32[32,128,128]{1,2,0:T(8,128)} async-done(((f32[32,128,128]{1,2,0:T(8,128)}), f32[32,128,128]{1,2,0:T(8,128)}, u32[]{:S(2)}, u32[]{:S(2)}) %all-to-all-start.1) | async-done | bytes 2097184 | tf_op jit(solution)/shard_map/all_to_all | solution.py:129
  129.2 3.8 convolution_subtract_fusion
  135.5 3.6 fusion.12
  139.2 3.6 fusion.14
  142.7 4.2 subtract_multiply_fusion
  151.3 3.9 add_multiply_fusion
  167.5 4.1 all-to-all-start.2
  171.6 3.9 fusion.4
  175.6 3.4 fusion.45
  181.6 16.3 %all-to-all-done.2 = f32[128,32,64]{0,2,1:T(8,128)S(1)} async-done(((f32[128,32,64]{0,2,1:T(8,128)}), f32[128,32,64]{0,2,1:T(8,128)S(1)}, u32[]{:S(2)}, u32[]{:S(2)}) %all-to-all-start.2) | async-done | bytes 1048608 | tf_op jit(solution)/shard_map/all_to_all | solution.py:139
  197.8 4.0 all-to-all-start.3
  205.7 22.3 %all-to-all-done.3 = f32[128,32,64]{0,2,1:T(8,128)} async-done(((f32[128,32,64]{0,2,1:T(8,128)}), f32[128,32,64]{0,2,1:T(8,128)}, u32[]{:S(2)}, u32[]{:S(2)}) %all-to-all-start.3) | async-done | bytes 1048608 | tf_op jit(solution)/shard_map/all_to_all | solution.py:146
  238.4 3.5 collective-permute-done.1
  242.3 4.3 collective-permute-start.2
  250.8 43.0 %all-reduce.8 = (f32[]{:T(128)}, f32[]{:T(128)}) all-reduce(f32[]{:T(128)} %get-tuple-element.10, f32[]{:T(128)} %get-tuple-element.9), channel_id=1, replica_groups=mesh['strip'=32] {'strip'}, use_global_device_ids=true, to_apply=%region_1.2 | all-reduce | flops 2 | bytes 16 | tf_op jit(solution)/shard_map/psum | solution.py:182
  298.9 4.3 collective-permute-done.5
  305.1 41.9 %all-reduce.7 = (f32[]{:T(128)}, f32[]{:T(128)}) all-reduce(f32[]{:T(128)} %get-tuple-element.8, f32[]{:T(128)} %get-tuple-element.7), channel_id=1, replica_groups=mesh['strip'=32] {'strip'}, use_global_device_ids=true, to_apply=%region_5.6 | all-reduce | flops 2 | bytes 16 | tf_op jit(solution)/shard_map/psum | solution.py:182
  357.1 4.3 collective-permute-done.7
  361.4 4.3 multiply_reduce_fusion.1
  365.7 41.8 %all-reduce.6 = (f32[]{:T(128)}, f32[]{:T(128)}) all-reduce(f32[]{:T(128)} %get-tuple-element.6, f32[]{:T(128)} %get-tuple-element.5), channel_id=1, replica_groups=mesh['strip'=32] {'strip'}, use_global_device_ids=true, to_apply=%region_9.10 | all-reduce | flops 2 | bytes 16 | tf_op jit(solution)/shard_map/psum | solution.py:182
  415.9 4.2 collective-permute-done.9
  421.2 41.9 %all-reduce.5 = (f32[]{:T(128)}, f32[]{:T(128)}) all-reduce(f32[]{:T(128)} %get-tuple-element.4, f32[]{:T(128)} %get-tuple-element.3), channel_id=1, replica_groups=mesh['strip'=32] {'strip'}, use_global_device_ids=true, to_apply=%region_13.14 | all-reduce | flops 2 | bytes 16 | tf_op jit(solution)/shard_map/psum | solution.py:182
  468.8 16.6 %gather_fusion = f32[2048]{0:T(1024)S(1)} fusion(f32[64,2048]{1,0:T(8,128)S(1)} %multiply_add_fusion.1, s32[2048]{0:T(1024)S(1)} %fusion.195), kind=kCustom, calls=%fused_computation | custom fusion | bytes 32768 | tf_op jit(solution)/shard_map/gather | solution.py:201
  486.1 40.2 %psum.71 = f32[]{:T(128)} all-reduce(f32[]{:T(128)} %multiply_reduce_fusion.7), channel_id=1, replica_groups=mesh['strip'=32] {'strip'}, use_global_device_ids=true, to_apply=%region_17.18 | all-reduce | flops 1 | bytes 8 | tf_op jit(solution)/shard_map/psum | solution.py:203
  (85 shorter events, 74.8 us)
Async XLA Ops:
  8.6 3.6 copy-start.2
  17.5 56.2 %all-to-all-start = ((f32[32,128,128]{1,2,0:T(8,128)}), f32[32,128,128]{1,2,0:T(8,128)}, u32[]{:S(2)}, u32[]{:S(2)}) async-start(f32[32,128,128]{1,2,0:T(8,128)} %subtract_bitcast_fusion), calls=%async_computation | async-start | bytes 4194304 | tf_op jit(solution)/shard_map/all_to_all | solution.py:128
  73.7 52.9 %all-to-all-start.1 = ((f32[32,128,128]{1,2,0:T(8,128)}), f32[32,128,128]{1,2,0:T(8,128)}, u32[]{:S(2)}, u32[]{:S(2)}) async-start(f32[32,128,128]{1,2,0:T(8,128)} %add_bitcast_fusion), calls=%async_computation.1 | async-start | bytes 4194304 | tf_op jit(solution)/shard_map/all_to_all | solution.py:129
  129.2 3.8 copy-start.3
  159.9 1.3 copy-start.1
  167.5 30.3 %all-to-all-start.2 = ((f32[128,32,64]{0,2,1:T(8,128)}), f32[128,32,64]{0,2,1:T(8,128)S(1)}, u32[]{:S(2)}, u32[]{:S(2)}) async-start(f32[128,32,64]{0,2,1:T(8,128)} %bitcast.183), calls=%async_computation.2 | async-start | bytes 2097152 | tf_op jit(solution)/shard_map/all_to_all | solution.py:139
  197.8 30.1 %all-to-all-start.3 = ((f32[128,32,64]{0,2,1:T(8,128)}), f32[128,32,64]{0,2,1:T(8,128)}, u32[]{:S(2)}, u32[]{:S(2)}) async-start(f32[128,32,64]{0,2,1:T(8,128)} %bitcast.33), calls=%async_computation.3 | async-start | bytes 2097152 | tf_op jit(solution)/shard_map/all_to_all | solution.py:146
  233.9 7.9 %copy-start.7 = (f32[64,2048]{1,0:T(8,128)S(1)}, f32[64,2048]{1,0:T(8,128)}, u32[]{:S(2)}) copy-start(f32[64,2048]{1,0:T(8,128)} %param.13) | copy-start | bytes 1572868
  235.8 2.6 collective-permute-start
  237.1 4.8 collective-permute-start.1
  242.3 5.6 %collective-permute-start.2 = (f32[1,2048]{1,0:T(1,128)S(1)}, f32[1,2048]{1,0:T(1,128)S(1)}, u32[]{:S(2)}, u32[]{:S(2)}) collective-permute-start(f32[1,2048]{1,0:T(1,128)S(1)} %get-tuple-element.46), channel_id=1, source_target_pairs={{0,1},{1,2},{2,3},{3,4},{4,5},{5,6},{6,7},{7,8},{8,9},{9,10},{10,1... | collective-permute-start | bytes 24584 | tf_op jit(solution)/shard_map/ppermute | solution.py:19
  246.6 3.1 collective-permute-start.3
  296.2 6.9 %copy-start.4 = (f32[64,2048]{1,0:T(8,128)}, f32[64,2048]{1,0:T(8,128)S(1)}, u32[]{:S(2)}) copy-start(f32[64,2048]{1,0:T(8,128)S(1)} %get-tuple-element.25) | copy-start | bytes 1572868
  296.2 8.9 %copy-start.8 = (f32[64,2048]{1,0:T(8,128)}, f32[64,2048]{1,0:T(8,128)S(1)}, u32[]{:S(2)}) copy-start(f32[64,2048]{1,0:T(8,128)S(1)} %get-tuple-element.26) | copy-start | bytes 1572868
  296.2 2.6 collective-permute-start.4
  297.5 5.6 %collective-permute-start.5 = (f32[1,2048]{1,0:T(1,128)S(1)}, f32[1,2048]{1,0:T(1,128)S(1)}, u32[]{:S(2)}, u32[]{:S(2)}) collective-permute-start(f32[1,2048]{1,0:T(1,128)S(1)} %get-tuple-element.45), channel_id=1, source_target_pairs={{1,0},{2,1},{3,2},{4,3},{5,4},{6,5},{7,6},{8,7},{9,8},{10,9},{11,1... | collective-permute-start | bytes 24584 | tf_op jit(solution)/shard_map/ppermute | solution.py:22
  353.7 0.8 copy-start.5
  354.5 2.6 collective-permute-start.6
  355.8 5.6 %collective-permute-start.7 = (f32[1,2048]{1,0:T(1,128)S(1)}, f32[1,2048]{1,0:T(1,128)S(1)}, u32[]{:S(2)}, u32[]{:S(2)}) collective-permute-start(f32[1,2048]{1,0:T(1,128)S(1)} %get-tuple-element.43), channel_id=1, source_target_pairs={{1,0},{2,1},{3,2},{4,3},{5,4},{6,5},{7,6},{8,7},{9,8},{10,9},{11,1... | collective-permute-start | bytes 24584 | tf_op jit(solution)/shard_map/ppermute | solution.py:22
  365.7 50.1 %copy-start.9 = (s32[2048]{0:T(1024)S(1)}, s32[2048]{0:T(1024)}, u32[]{:S(2)}) copy-start(s32[2048]{0:T(1024)} %param.14) | copy-start | bytes 24580
  413.2 8.0 %copy-start.6 = (f32[64,2048]{1,0:T(8,128)}, f32[64,2048]{1,0:T(8,128)S(1)}, u32[]{:S(2)}) copy-start(f32[64,2048]{1,0:T(8,128)S(1)} %get-tuple-element.19) | copy-start | bytes 1572868
  413.2 2.6 collective-permute-start.8
  414.5 5.6 %collective-permute-start.9 = (f32[1,2048]{1,0:T(1,128)S(1)}, f32[1,2048]{1,0:T(1,128)S(1)}, u32[]{:S(2)}, u32[]{:S(2)}) collective-permute-start(f32[1,2048]{1,0:T(1,128)S(1)} %get-tuple-element.41), channel_id=1, source_target_pairs={{1,0},{2,1},{3,2},{4,3},{5,4},{6,5},{7,6},{8,7},{9,8},{10,9},{11,1... | collective-permute-start | bytes 24584 | tf_op jit(solution)/shard_map/ppermute | solution.py:22
  468.7 16.7 %copy-start = (f32[64,2048]{1,0:T(8,128)}, f32[64,2048]{1,0:T(8,128)S(1)}, u32[]{:S(2)}) copy-start(f32[64,2048]{1,0:T(8,128)S(1)} %multiply_add_fusion.1) | copy-start | bytes 1572868
  468.8 16.7 %copy-start.10 = (f32[2048]{0:T(1024)S(1)}, f32[2048]{0:T(1024)}, u32[]{:S(2)}) copy-start(f32[2048]{0:T(1024)} %param.15) | copy-start | bytes 24580
where the time goes:
time: 539 us; the launch traced here: 528 us
  blocking collectives  209 us (39%)
  waiting for transfers between devices  133 us (25%)
  matrix products  79.3 us (15%)
  starting transfers between devices  35.6 us (7%)
  local copies, waits for them, and re-layouts  33.2 us (6%)
  between operations  19.5 us (4%)
  other arithmetic  18.7 us (3%)
    psum x4, blocking collectives, body(): lax.psum((jnp.sum(residual * precond), jnp.sum(precond * image)), 'strip')  169 us
    psum x1, blocking collectives, body(): total = lax.psum(jnp.sum(differ * differ), 'strip')  40.2 us
    all_to_all x1, waiting for transfers between devices, body(): lax.all_to_all(send_real, 'strip', split_axis=0, concat_axis=2, tiled=True)  38.6 us
    all_to_all x1, waiting for transfers between devices, body(): lax.all_to_all(send_imag, 'strip', split_axis=0, concat_axis=2, tiled=True)  38.2 us
    all_to_all x1, waiting for transfers between devices, body(): lax.all_to_all(field_imag.reshape(width, parts, field_rows), 'strip', spl...  22.3 us
    ppermute x5, waiting for transfers between devices, padded(): lax.ppermute(lax.slice_in_dim(block, 0, width, axis=dim), axis, backward)  18 us
    gather x1, local copies, waits for them, and re-layouts, body(): picked = pressure[jnp.clip(local_row, 0, field_rows - 1), cell_col]  16.6 us
    all_to_all x1, waiting for transfers between devices, body(): lax.all_to_all(field_real.reshape(width, parts, field_rows), 'strip', spl...  16.3 us
  transfers between devices with their start and end apart: 14, of which 9 were waited for; matrix products, arithmetic and copies ran while one was open for 6% of the time, Pallas kernels for 0%

commit v1 on v0

v1 whole, which is shorter than its diff:
```python
import functools
import math

import jax
import jax.numpy as jnp
import numpy as np
from jax import lax
from jax.experimental import pallas as pl
from jax.experimental.pallas import tpu as pltpu
from jax.sharding import PartitionSpec as P

ITERS = 4
LANES = 128
HALO = 8
TERMS = 2 * ITERS
PAIRS = [(i, j) for i in range(ITERS) for j in range(i, ITERS)]
SUMS = TERMS + len(PAIRS) + ITERS


def mm(left, right):
    return lax.dot_general(
        left,
        right,
        (((1,), (0,)), ((), ())),
        precision=lax.Precision.HIGHEST,
        preferred_element_type=jnp.float32,
    )


def dft_tables():
    spot = np.arange(LANES)
    angle = 2.0 * np.pi * np.outer(spot, spot) / LANES
    cos, sin = np.cos(angle), np.sin(angle)
    forward = np.block([[cos, -sin], [sin, cos]])
    inverse = np.block([[cos, sin], [-sin, cos]])
    half = LANES // 2
    whole = 2.0 * np.pi * np.outer(spot, np.arange(1, half)) / LANES
    edge = np.ones((LANES, 1))
    alternate = ((-1.0) ** spot)[:, None]
    zero_f = np.concatenate([edge, np.cos(whole), alternate, -np.sin(whole)], 1)
    zero_i = np.concatenate([edge, 2 * np.cos(whole), alternate, -2 * np.sin(whole)], 1).T
    odd = 2.0 * np.pi * np.outer(spot, np.arange(half) + 0.5) / LANES
    half_f = np.concatenate([np.cos(odd), -np.sin(odd)], 1)
    half_i = 2.0 * np.concatenate([np.cos(odd), -np.sin(odd)], 1).T
    none = np.zeros((LANES, LANES))
    special_f = np.block([[zero_f, none], [none, half_f]])
    special_i = np.block([[zero_i, none], [none, half_i]])
    return forward, inverse, special_f, special_i


def twiddle_table(length, factor):
    angle = 2.0 * np.pi * np.outer(np.arange(factor // 2), np.arange(LANES)) / length
    return np.cos(angle), np.sin(angle)


def times(value, factor):
    if value is None or factor == 0.0:
        return None
    if factor == 1.0:
        return value
    if factor == -1.0:
        return -value
    return value * factor


def plus(left, right):
    if left is None:
        return right
    if right is None:
        return left
    return left + right


def minus(left, right):
    if right is None:
        return left
    if left is None:
        return -right
    return left - right


def root(k, n):
    quarter = (8 * k) % (8 * n)
    if quarter % n == 0 and (quarter // n) % 2 == 0:
        return ((1.0, 0.0), (0.0, 1.0), (-1.0, 0.0), (0.0, -1.0))[(quarter // n) // 2]
    return (math.cos(2 * math.pi * k / n), math.sin(2 * math.pi * k / n))


def rotate(re, im, c, s):
    return (
        minus(times(re, c), times(im, s)),
        plus(times(re, s), times(im, c)),
    )


def rfft(values):
    n = len(values)
    if n == 2:
        return [(values[0] + values[1], None), (values[0] - values[1], None)]
    even = rfft(values[0::2])
    odd = rfft(values[1::2])
    out = [None] * (n // 2 + 1)
    for k in range(n // 4 + 1):
        c, s = root(k, n)
        tr, ti = rotate(odd[k][0], odd[k][1], c, -s)
        er, ei = even[k]
        out[k] = (plus(er, tr), plus(ei, ti))
        if k != n // 4:
            out[n // 2 - k] = (minus(er, tr), minus(ti, ei))
    return out


def irfft(spectrum, n):
    if n == 2:
        return [spectrum[0][0] + spectrum[1][0]]
    even, odd = [], []
    for k in range(n // 4 + 1):
        ar, ai = spectrum[k]
        br, bi = spectrum[n // 2 - k]
        if k == n // 4:
            even.append((2.0 * ar, None))
            odd.append((-2.0 * ai, None))
            continue
        even.append((plus(ar, br), minus(ai, bi)))
        c, s = root(k, n)
        odd.append(rotate(minus(ar, br), plus(ai, bi), c, s))
    even = irfft(even, n // 2)
    odd = irfft(odd, n // 2)
    return [value for pair in zip(even, odd) for value in pair]


def row_kernel(step, state, noise, twiddle, pair_w, special_w, out, work, *, factor):
    rows = state.shape[0]
    half = factor // 2
    rate = step[0]
    keep = jnp.sqrt(jnp.full((8, LANES), 1.0 - rate * rate, jnp.float32))

    def group(index, carry):
        base = pl.multiple_of(index * 8, 8)
        tiles = [
            keep * state[pl.ds(base, 8), LANES * a : LANES * (a + 1)]
            + rate * noise[pl.ds(base, 8), LANES * a : LANES * (a + 1)]
            for a in range(factor)
        ]
        spectrum = rfft(tiles)
        work[0, pl.ds(base, 8), :LANES] = spectrum[0][0]
        work[0, pl.ds(base, 8), LANES:] = spectrum[half][0]
        for j in range(1, half):
            c = twiddle[j : j + 1, :]
            s = twiddle[half + j : half + j + 1, :]
            re, im = spectrum[j]
            work[j, pl.ds(base, 8), :LANES] = re * c + im * s
            work[j, pl.ds(base, 8), LANES:] = im * c - re * s
        return carry

    lax.fori_loop(0, rows // 8, group, 0)
    first = mm(work[0], special_w[...])
    out[0] = first[:, :LANES]
    out[1] = first[:, LANES:]
    for j in range(1, half):
        value = mm(work[j], pair_w[...])
        out[2 * j] = value[:, :LANES]
        out[2 * j + 1] = value[:, LANES:]


def row_forward(state, noise, step, tables):
    rows, length = state.shape
    factor = length // LANES
    block = min(32, rows)
    twiddle, pair_w, special_w = tables
    whole = lambda i: (0, 0)
    return pl.pallas_call(
        functools.partial(row_kernel, factor=factor),
        grid=(rows // block,),
        in_specs=[
            pl.BlockSpec(memory_space=pltpu.SMEM),
            pl.BlockSpec((block, length), lambda i: (i, 0)),
            pl.BlockSpec((block, length), lambda i: (i, 0)),
            pl.BlockSpec(twiddle.shape, whole),
            pl.BlockSpec(pair_w.shape, whole),
            pl.BlockSpec(special_w.shape, whole),
        ],
        out_specs=pl.BlockSpec((factor, block, LANES), lambda i: (0, i, 0)),
        out_shape=jax.ShapeDtypeStruct((factor, rows, LANES), jnp.float32),
        scratch_shapes=[pltpu.VMEM((factor // 2, block, 2 * LANES), jnp.float32)],
        name="row_forward",
    )(step, state, noise, twiddle, pair_w, special_w)


def column_kernel(
    scale, column, table, forward_w, special_f, inverse_w, special_i, wave, out, work, field, *, field_rows
):
    factor, _, width = column.shape
    half = factor // 2
    length = factor * LANES
    parts = out.shape[0]

    def ahead(index, carry):
        base = pl.multiple_of(index * 8, 8)
        spectrum = rfft([column[a, pl.ds(base, 8), :] for a in range(factor)])
        low = pl.ds(base, 8)
        high = pl.ds(pl.multiple_of(base + LANES, 8), 8)
        work[0, low, :] = spectrum[0][0]
        work[0, high, :] = spectrum[half][0]
        turn = table[low, :]
        for j in range(1, half):
            c = turn[:, j : j + 1]
            s = turn[:, half + j : half + j + 1]
            re, im = spectrum[j]
            work[j, low, :] = re * c + im * s
            work[j, high, :] = im * c - re * s
        return carry

    lax.fori_loop(0, LANES // 8, ahead, 0)
    place = lax.broadcasted_iota(jnp.int32, (LANES, width), 0)
    side = wave[...] + scale[1]
    gain = scale[0]

    def amplitude(freq):
        freq = jnp.minimum(freq, length - freq).astype(jnp.float32)
        return gain / (freq * freq + side)

    for j in range(half):
        if j == 0:
            value = mm(special_f[...], work[0])
            halves = LANES // 2
            top = amplitude(factor * jnp.where(place > halves, place - halves, place))
            low = amplitude(half + factor * jnp.where(place >= halves, place - halves, place))
            value = jnp.concatenate([value[:LANES] * top, value[LANES:] * low], axis=0)
            work[0] = mm(special_i[...], value)
        else:
            value = mm(forward_w[...], work[j])
            top = amplitude(j + factor * place)
            value = jnp.concatenate([value[:LANES] * top, value[LANES:] * top], axis=0)
            work[j] = mm(inverse_w[...], value)

    rim = jnp.zeros((HALO, width), jnp.float32)
    field[:HALO, :] = rim
    field[HALO + length // 2 :, :] = rim

    def back(index, carry):
        base = pl.multiple_of(index * 8, 8)
        low = pl.ds(base, 8)
        high = pl.ds(pl.multiple_of(base + LANES, 8), 8)
        turn = table[low, :]
        spectrum = [(work[0, low, :], None)]
        for j in range(1, half):
            c = turn[:, j : j + 1]
            s = turn[:, half + j : half + j + 1]
            re, im = work[j, low, :], work[j, high, :]
            spectrum.append((re * c - im * s, re * s + im * c))
        spectrum.append((work[0, high, :], None))
        values = irfft(spectrum, factor)
        for a in range(half):
            field[pl.ds(pl.multiple_of(base + HALO + LANES * a, 8), 8), :] = values[a]
        return carry

    lax.fori_loop(0, LANES // 8, back, 0)
    for part in range(parts):
        out[part] = field[field_rows * part : field_rows * (part + 1) + 2 * HALO, :]


def column_filter(column, scale, wave, tables, parts, field_rows):
    factor, _, width = column.shape
    length = factor * LANES
    vmem = pl.BlockSpec(memory_space=pltpu.VMEM)
    return pl.pallas_call(
        functools.partial(column_kernel, field_rows=field_rows),
        in_specs=[pl.BlockSpec(memory_space=pltpu.SMEM)] + [vmem] * 7,
        out_specs=vmem,
        out_shape=jax.ShapeDtypeStruct((parts, field_rows + 2 * HALO, width), jnp.float32),
        scratch_shapes=[
            pltpu.VMEM((factor // 2, 2 * LANES, width), jnp.float32),
            pltpu.VMEM((length // 2 + 2 * HALO, width), jnp.float32),
        ],
        name="column_filter",
    )(scale, column, *tables, wave)


def observe_kernel(local, cells, values, count, total, left):
    rows, columns = count.shape
    block = columns
    origin = pl.program_id(0) * block

    @pl.when(pl.program_id(0) == 0)
    def _():
        row = lax.broadcasted_iota(jnp.int32, (rows, local.shape[1]), 0)
        here = row == local[...]
        value = jnp.broadcast_to(values[...], here.shape)
        first = value.astype(jnp.bfloat16).astype(jnp.float32)
        second = (value - first).astype(jnp.bfloat16).astype(jnp.float32)
        third = value - first - second
        for slot, piece in enumerate((1.0, first, second, third)):
            left[slot * rows : (slot + 1) * rows, :] = jnp.where(here, piece, 0.0).astype(jnp.bfloat16)

    spot = lax.broadcasted_iota(jnp.int32, (block, local.shape[1]), 0) + origin
    right = jnp.where(spot == cells[...], 1.0, 0.0).astype(jnp.bfloat16)
    result = lax.dot_general(
        left[...], right, (((1,), (1,)), ((), ())), preferred_element_type=jnp.float32
    )
    count[...] = result[:rows]
    total[...] = (result[3 * rows :] + result[2 * rows : 3 * rows]) + result[rows : 2 * rows]


def observe(local_row, cell_col, values, rows, columns):
    number = values.shape[1]
    block = 256
    whole = pl.BlockSpec((1, number), lambda i: (0, 0))
    piece = pl.BlockSpec((rows, block), lambda i: (0, i))
    shape = jax.ShapeDtypeStruct((rows, columns), jnp.float32)
    return pl.pallas_call(
        observe_kernel,
        grid=(columns // block,),
        in_specs=[whole, whole, whole],
        out_specs=(piece, piece),
        out_shape=(shape, shape),
        scratch_shapes=[pltpu.VMEM((4 * rows, number), jnp.bfloat16)],
        cost_estimate=pl.CostEstimate(
            flops=8 * rows * number * columns, transcendentals=0, bytes_accessed=8 * rows * columns
        ),
        name="observe",
    )(local_row, cell_col, values)


def two_sum(a, b):
    s = a + b
    t = s - a
    return s, (a - (s - t)) + (b - t)


def split(a):
    t = a * 4097.0
    high = t - (t - a)
    return high, a - high


def two_prod(a, b):
    p = a * b
    ah, al = split(a)
    bh, bl = split(b)
    return p, ((ah * bh - p) + ah * bl + al * bh) + al * bl


def dd_add(x, y):
    s, e = two_sum(x[0], y[0])
    e = e + (x[1] + y[1])
    high = s + e
    return high, e - (high - s)


def dd_neg(x):
    return -x[0], -x[1]


def dd_mul(x, y):
    p, e = two_prod(x[0], y[0])
    e = e + (x[0] * y[1] + x[1] * y[0])
    high = p + e
    return high, e - (high - p)


def dd_div(x, y):
    first = x[0] / y[0]
    rest = dd_add(x, dd_neg(dd_mul(y, (first, jnp.zeros_like(first)))))
    second = rest[0] / y[0]
    rest = dd_add(rest, dd_neg(dd_mul(y, (second, jnp.zeros_like(first)))))
    third = rest[0] / y[0]
    high, low = two_sum(first, second)
    return dd_add((high, low), (third, jnp.zeros_like(third)))


def fold(high, low, shift, axis):
    other, error = two_sum(high, pltpu.roll(high, shift, axis))
    return other, (low + pltpu.roll(low, shift, axis)) + error


def tile_sum(value):
    pieces = [value[:, LANES * i : LANES * (i + 1)] for i in range(value.shape[1] // LANES)]
    while len(pieces) > 1:
        pieces = [a + b for a, b in zip(pieces[0::2], pieces[1::2])]
    return pieces[0]


def krylov_kernel(
    origin, coefs, source, count, total, twiddle, inverse_w, special_i,
    log_perm, basis, partial,
    work, kappa, centre, inverse, north, south, west, east, vector,
):
    factor, extent, _ = coefs.shape
    half = factor // 2
    columns = half * LANES
    rows = extent - 2 * HALO
    groups = extent // 8
    pair = jnp.concatenate([coefs[0], coefs[1]], axis=1)
    work[0] = mm(pair, special_i[...])
    for j in range(1, half):
        pair = jnp.concatenate([coefs[2 * j], coefs[2 * j + 1]], axis=1)
        work[j] = mm(pair, inverse_w[...])

    rim = jnp.zeros((8, columns), jnp.float32)
    for ref in (kappa, vector.at[0], vector.at[1]):
        ref[:8, :] = rim
        ref[8 + extent :, :] = rim

    first_row = origin[0] - HALO
    limit = origin[1]

    def inverse_group(index, carry):
        base = pl.multiple_of(index * 8, 8)
        low = pl.ds(base, 8)
        spectrum = [(work[0, low, :LANES], None)]
        for j in range(1, half):
            c = twiddle[j : j + 1, :]
            s = twiddle[half + j : half + j + 1, :]
            re, im = work[j, low, :LANES], work[j, low, LANES:]
            spectrum.append((re * c - im * s, re * s + im * c))
        spectrum.append((work[0, low, LANES:], None))
        values = irfft(spectrum, factor)
        row = lax.broadcasted_iota(jnp.int32, (8, LANES), 0) + (base + first_row)
        valid = (row >= 0) & (row < limit)
        store = pl.ds(pl.multiple_of(base + 8, 8), 8)
        for a in range(half):
            kappa[store, LANES * a : LANES * (a + 1)] = jnp.where(valid, jnp.exp(values[a]), 0.0)

        @pl.when((index >= HALO // 8) & (index < groups - HALO // 8))
        def _():
            own = pl.ds(pl.multiple_of(base - HALO, 8), 8)
            for a in range(half):
                log_perm[own, LANES * a : LANES * (a + 1)] = values[a]

        return carry

    lax.fori_loop(0, groups, inverse_group, 0)

    lane = lax.broadcasted_iota(jnp.int32, (8, columns), 1)
    inner_west = lane > 0
    inner_east = lane < columns - 1
    zero = jnp.zeros((8, LANES), jnp.float32)
    sums = [zero] * SUMS

    for group in range(groups):
        at = 8 + 8 * group
        own = HALO // 8 <= group < groups - HALO // 8
        here = kappa[at : at + 8, :]
        up = 0.5 * (here + kappa[at - 1 : at + 7, :])
        down = 0.5 * (here + kappa[at + 1 : at + 9, :])
        left = jnp.where(inner_west, pltpu.roll(here, 1, 1), 0.0)
        right = jnp.where(inner_east, pltpu.roll(here, columns - 1, 1), 0.0)
        left = 0.5 * (here + left)
        right = 0.5 * (here + right)
        middle = up + down + left + right
        row = lax.broadcasted_iota(jnp.int32, (8, columns), 0) + (8 * group + first_row)
        rest = jnp.where((row >= 0) & (row < limit), 1.0 / middle, 0.0)
        put = slice(8 * group, 8 * group + 8)
        centre[put, :] = middle
        inverse[put, :] = rest
        north[put, :] = up
        south[put, :] = down
        west[put, :] = jnp.where(inner_west, left, 0.0)
        east[put, :] = jnp.where(inner_east, right, 0.0)
        first = source[put, :]
        value = first * rest
        vector[0, at : at + 8, :] = value
        if own:
            basis[0, 8 * group - HALO : 8 * group - HALO + 8, :] = value
            sums[0] = sums[0] + tile_sum(first * value)

    for step in range(ITERS):
        now = vector.at[step % 2]
        new = vector.at[(step + 1) % 2]
        for group in range(groups):
            at = 8 + 8 * group
            own = HALO // 8 <= group < groups - HALO // 8
            if step == ITERS - 1 and not own:
                continue
            put = slice(8 * group, 8 * group + 8)
            here = now[at : at + 8, :]
            image = (
                centre[put, :] * here
                - north[put, :] * now[at - 1 : at + 7, :]
                - south[put, :] * now[at + 1 : at + 9, :]
                - west[put, :] * pltpu.roll(here, 1, 1)
                - east[put, :] * pltpu.roll(here, columns - 1, 1)
            )
            if own:
                sums[2 * step + 1] = sums[2 * step + 1] + tile_sum(here * image)
            if step < ITERS - 1:
                value = image * inverse[put, :]
                new[at : at + 8, :] = value
                if own:
                    basis[step + 1, 8 * group - HALO : 8 * group - HALO + 8, :] = value
                    sums[2 * step + 2] = sums[2 * step + 2] + tile_sum(value * image)

    for group in range(rows // 8):
        put = slice(8 * group, 8 * group + 8)
        vectors = [basis[k, put, :] for k in range(ITERS)]
        weight = count[put, :]
        weighted = [weight * v for v in vectors]
        for spot, (i, j) in enumerate(PAIRS):
            sums[TERMS + spot] = sums[TERMS + spot] + tile_sum(weighted[i] * vectors[j])
        datum = total[put, :]
        for k in range(ITERS):
            slot = TERMS + len(PAIRS) + k
            sums[slot] = sums[slot] + tile_sum(datum * vectors[k])

    sub = lax.broadcasted_iota(jnp.int32, (8, LANES), 0)
    spot = lax.broadcasted_iota(jnp.int32, (8, LANES), 1)
    row = zero
    for begin in range(0, SUMS, 8):
        high, low = zero, zero
        for k in range(begin, min(begin + 8, SUMS)):
            h, e = sums[k], zero
            for shift in (4, 2, 1):
                h, e = fold(h, e, shift, 0)
            high = jnp.where(sub == k - begin, h, high)
            low = jnp.where(sub == k - begin, e, low)
        for shift in (64, 32, 16, 8, 4, 2, 1):
            high, low = fold(high, low, shift, 1)
        row = row + jnp.where(spot == sub + begin, high, 0.0)
        row = row + jnp.where(spot == sub + begin + LANES // 2, low, 0.0)
    for shift in (4, 2, 1):
        row = row + pltpu.roll(row, shift, 0)
    for part in range(partial.shape[0]):
        partial[part] = row[:1]


def krylov(origin, coefs, source, count, total, tables, parts):
    factor, extent, _ = coefs.shape
    columns = factor // 2 * LANES
    rows = extent - 2 * HALO
    vmem = pl.BlockSpec(memory_space=pltpu.VMEM)
    plane = pltpu.VMEM((extent, columns), jnp.float32)
    padded = pltpu.VMEM((extent + 16, columns), jnp.float32)
    return pl.pallas_call(
        krylov_kernel,
        in_specs=[pl.BlockSpec(memory_space=pltpu.SMEM)] + [vmem] * 7,
        out_specs=(vmem, vmem, vmem),
        out_shape=(
            jax.ShapeDtypeStruct((rows, columns), jnp.float32),
            jax.ShapeDtypeStruct((ITERS, rows, columns), jnp.float32),
            jax.ShapeDtypeStruct((parts, 1, LANES), jnp.float32),
        ),
        scratch_shapes=[
            pltpu.VMEM((factor // 2, extent, 2 * LANES), jnp.float32),
            padded,
            plane,
            plane,
            plane,
            plane,
            plane,
            plane,
            pltpu.VMEM((2, extent + 16, columns), jnp.float32),
        ],
        name="krylov",
    )(origin, coefs, source, count, total, *tables)


def final_kernel(partial, basis, values, pressure, loglik):
    parts = partial.shape[0]
    high = jnp.concatenate([partial[k] for k in range(parts)], axis=0)
    low = pltpu.roll(high, LANES // 2, 1)
    while high.shape[0] > 8:
        middle = high.shape[0] // 2
        top, error = two_sum(high[:middle], high[middle:])
        low = (low[:middle] + low[middle:]) + error
        high = top
    for shift in (4, 2, 1):
        high, low = fold(high, low, shift, 0)

    def pick(k):
        return (
            jnp.broadcast_to(high[:, k : k + 1], (8, LANES)),
            jnp.broadcast_to(low[:, k : k + 1], (8, LANES)),
        )

    moments = [pick(k) for k in range(TERMS)]
    matrix = [[moments[i + j + 1] for j in range(ITERS)] for i in range(ITERS)]
    right = [moments[i] for i in range(ITERS)]
    for i in range(ITERS):
        for r in range(i + 1, ITERS):
            ratio = dd_neg(dd_div(matrix[i][r], matrix[i][i]))
            for c in range(r, ITERS):
                matrix[r][c] = dd_add(matrix[r][c], dd_mul(ratio, matrix[i][c]))
            right[r] = dd_add(right[r], dd_mul(ratio, right[i]))
    weights = [None] * ITERS
    for i in reversed(range(ITERS)):
        value = right[i]
        for c in range(i + 1, ITERS):
            value = dd_add(value, dd_neg(dd_mul(matrix[i][c], weights[c])))
        weights[i] = dd_div(value, matrix[i][i])

    data = values[...]
    h, e = two_prod(data, data)
    while h.shape[0] > 8:
        middle = h.shape[0] // 2
        top, error = two_sum(h[:middle], h[middle:])
        e = (e[:middle] + e[middle:]) + error
        h = top
    for shift in (4, 2, 1):
        h, e = fold(h, e, shift, 0)
    for shift in (64, 32, 16, 8, 4, 2, 1):
        h, e = fold(h, e, shift, 1)
    misfit = (h, e)
    for spot, (i, j) in enumerate(PAIRS):
        term = dd_mul(dd_mul(weights[i], weights[j]), pick(TERMS + spot))
        misfit = dd_add(misfit, term)
        if i != j:
            misfit = dd_add(misfit, term)
    for k in range(ITERS):
        term = dd_neg(dd_mul(weights[k], pick(TERMS + len(PAIRS) + k)))
        misfit = dd_add(misfit, dd_add(term, term))
    number = values.shape[0] * LANES
    loglik[...] = (-(2.0 / number) * (misfit[0] + misfit[1]))[:1, :]

    factors = [w[0][:1, :1] for w in weights]
    for group in range(pressure.shape[0] // 8):
        put = slice(8 * group, 8 * group + 8)
        value = factors[0] * basis[0, put, :]
        for k in range(1, ITERS):
            value = value + factors[k] * basis[k, put, :]
        pressure[put, :] = value


def finish(partial, basis, values):
    vmem = pl.BlockSpec(memory_space=pltpu.VMEM)
    return pl.pallas_call(
        final_kernel,
        in_specs=[vmem] * 3,
        out_specs=(vmem, vmem),
        out_shape=(
            jax.ShapeDtypeStruct(basis.shape[1:], jnp.float32),
            jax.ShapeDtypeStruct((1, LANES), jnp.float32),
        ),
        name="finish",
    )(partial, basis, values)


def exchange(block):
    return lax.all_to_all(block, "strip", split_axis=0, concat_axis=0, tiled=True)


def body(state, noise, step, field_scale, wave_scale, source, obs_cells, obs_values):
    parts = lax.axis_size("strip")
    position = lax.axis_index("strip")
    rows_here, length = state.shape
    factor = length // LANES
    half = factor // 2
    width = length // parts
    ways = parts // factor
    field_rows, columns = source.shape

    forward, inverse, special_f, special_i = (np.float32(t) for t in dft_tables())
    cos, sin = twiddle_table(length, factor)
    across = np.float32(np.concatenate([cos, sin], 0))
    down = np.zeros((LANES, LANES), np.float32)
    down[:, :factor] = across.T

    ahead = [(i, i + 1) for i in range(parts - 1)]
    behind = [(b, a) for a, b in ahead]
    above = lax.ppermute(source[field_rows - HALO :], "strip", ahead)
    below = lax.ppermute(source[:HALO], "strip", behind)
    wide_source = jnp.concatenate([above, source, below], axis=0)

    cell_row = obs_cells // columns - position * field_rows
    count, total = observe(
        cell_row[None, :], (obs_cells % columns)[None, :], obs_values[None, :], field_rows, columns
    )

    tiles = row_forward(state, noise, step, (across, forward, special_f))
    if ways > 1:
        tiles = tiles.reshape(factor, rows_here, ways, width).transpose(0, 2, 1, 3)
        tiles = tiles.reshape(parts, rows_here, width)
    column = exchange(tiles).reshape(factor, LANES, width)

    slot = position * width + lax.broadcasted_iota(jnp.int32, (1, width), 1)
    tile, lane = slot // LANES, slot % LANES
    middle = LANES // 2
    freq = jnp.where(
        tile == 0,
        factor * jnp.where(lane > middle, lane - middle, lane),
        jnp.where(
            tile == 1,
            half + factor * jnp.where(lane >= middle, lane - middle, lane),
            tile // 2 + factor * lane,
        ),
    )
    freq = jnp.minimum(freq, length - freq).astype(jnp.float32)
    wave = wave_scale[0]
    gain = field_scale[0] * wave / (math.sqrt(math.pi) * length)
    scale = jnp.stack([gain, wave * wave])
    blocks = column_filter(
        column,
        scale,
        freq * freq,
        (down, forward.T, special_f.T, inverse.T, special_i.T),
        parts,
        field_rows,
    )
    coefs = exchange(blocks)
    extent = field_rows + 2 * HALO
    if ways > 1:
        coefs = coefs.reshape(factor, ways, extent, width).transpose(0, 2, 1, 3)
        coefs = coefs.reshape(factor, extent, LANES)

    origin = jnp.stack([position * field_rows, parts * field_rows]).astype(jnp.int32)
    log_perm, basis, partial = krylov(
        origin, coefs, wide_source, count, total, (across, inverse, special_i), parts
    )
    pressure, loglik = finish(exchange(partial), basis, obs_values.reshape(-1, LANES))
    return (log_perm, pressure, loglik[0, 0])


def solution(mesh):
    placed = (P("strip", None), P("strip", None), P(), P(), P(), P("strip", None), P(), P())
    return jax.shard_map(
        body,
        mesh=mesh,
        in_specs=placed,
        out_specs=(P("strip", None), P("strip", None), P()),
        check_vma=False,
    )
```

time: 539 us -> 147 us (0.27); the launches traced: 528 us -> 147 us
  blocking collectives: 209 us -> 11.4 us
  matrix products: 79.3 us -> 0 us
  waiting for transfers between devices: 133 us -> 66.5 us
  Pallas kernels: 0 us -> 45.7 us
  local copies, waits for them, and re-layouts: 33.2 us -> 2.42 us
  starting transfers between devices: 35.6 us -> 15 us
  between operations: 19.5 us -> 2.65 us
  other arithmetic: 18.7 us -> 3.28 us
    psum x5 -> x0, blocking collectives: 209 us -> none  [the longest x4 169 us: body(): lax.psum((jnp.sum(residual * precond), jnp.sum(precond * image)), 'strip')]
    dot_general x28 -> x0, matrix products: 79.3 us -> none  [the longest x2 9.5 us: forward_permuted(): jnp.einsum('ja,...ka->...kj', outer_cos, turned_real, precision=precise)]
    all_to_all x4 -> x2, waiting for transfers between devices: 115 us -> 66.5 us  [exchange(): lax.all_to_all(block, 'strip', split_axis=0, concat_axis=0, tiled=True)]
    pallas_call x0 -> x5, Pallas kernels: none -> 45.7 us  [the longest x1 14.5 us: column_filter(): pl.pallas_call(functools.partial(column_kernel, field_rows=field_rows), i...]
    ppermute x10 -> x2, waiting for transfers between devices: 18 us -> 0.01 us  [the longest x1 0.01 us: body(): above = lax.ppermute(source[field_rows - HALO:], 'strip', ahead)]
    gather x1 -> x0, local copies, waits for them, and re-layouts: 16.6 us -> none  [body(): picked = pressure[jnp.clip(local_row, 0, field_rows - 1), cell_col]]
    ppermute x10 -> x2, starting transfers between devices: 15.9 us -> 3.63 us  [the longest x1 2.16 us: body(): above = lax.ppermute(source[field_rows - HALO:], 'strip', ahead)]
    all_to_all x0 -> x1, blocking collectives: none -> 11.4 us  [exchange(): lax.all_to_all(block, 'strip', split_axis=0, concat_axis=0, tiled=True)]
  transfers between devices with their start and end apart: 14 -> 4, of which waited for: 9 -> 2; matrix products, arithmetic and copies ran while one was open for 6% -> 2% of each run, Pallas kernels for 0% -> 4%
where the time goes in v1:
time: 147 us
  waiting for transfers between devices  66.5 us (45%)
  Pallas kernels  45.7 us (31%)
  starting transfers between devices  15 us (10%)
  blocking collectives  11.4 us (8%)
  other arithmetic  3.28 us (2%)
  between operations  2.65 us (2%)
  local copies, waits for them, and re-layouts  2.42 us (2%)
    all_to_all x2, waiting for transfers between devices, exchange(): lax.all_to_all(block, 'strip', split_axis=0, concat_axis=0, tiled=True)  66.5 us
    pallas_call x1, Pallas kernels, column_filter(): pl.pallas_call(functools.partial(column_kernel, field_rows=field_rows), i...  14.5 us
    pallas_call x1, Pallas kernels, row_forward(): pl.pallas_call(functools.partial(row_kernel, factor=factor), grid=(rows /...  12.1 us
    all_to_all x1, blocking collectives, exchange(): lax.all_to_all(block, 'strip', split_axis=0, concat_axis=0, tiled=True)  11.4 us
    all_to_all x2, starting transfers between devices, exchange(): lax.all_to_all(block, 'strip', split_axis=0, concat_axis=0, tiled=True)  11.4 us
    pallas_call x1, Pallas kernels, krylov(): pl.pallas_call(krylov_kernel, in_specs=[pl.BlockSpec(memory_space=pltpu.S...  9.95 us
    pallas_call x1, Pallas kernels, observe(): pl.pallas_call(observe_kernel, grid=(columns // block,), in_specs=[whole,...  5.93 us
    pallas_call x1, Pallas kernels, finish(): pl.pallas_call(final_kernel, in_specs=[vmem] * 3, out_specs=(vmem, vmem),...  3.18 us
  transfers between devices with their start and end apart: 4, of which 2 were waited for; matrix products, arithmetic and copies ran while one was open for 2% of the time, Pallas kernels for 4%

profile of v1, /device:TPU:0, one launch (start us, length us, event | category | flops | bytes accessed | tf_op | source)
XLA Modules:
  0.0 147.0 jit_solution(836069112524727505)
XLA Ops:
  1.3 12.1 %row_forward.1 = f32[32,128,128]{2,1,0:T(8,128)} custom-call(f32[1]{0:T(128)S(6)} %copy.21.step, f32[128,4096]{1,0:T(8,128)} %state.1, f32[128,4096]{1,0:T(8,128)} %noise.1, f32[32,128]{1,0:T(8,128)} %constant.101.clone.twiddle, f32[256,256]{1,0:T(8,128)} %constant.102.clone.pair_w.inverse_w, f32[256,256]{1,0:T(8,128)} %constant.103.clone.special_w), custom_call_target="tpu_custom_call" | custom-call | tf_op jit(solution)/shard_map/row_forward/pallas_call | solution.py:172
  13.4 7.3 %all-to-all-start = ((f32[32,128,128]{2,1,0:T(8,128)}), f32[32,128,128]{2,1,0:T(8,128)S(1)}, u32[]{:S(2)}, u32[]{:S(2)}) async-start(f32[32,128,128]{2,1,0:T(8,128)} %row_forward.1), calls=%async_computation | async-start | bytes 4194304 | tf_op jit(solution)/shard_map/all_to_all | solution.py:639
  22.0 0.5 fusion.4.wave
  22.6 0.6 pad_maximum_fusion.1.scale
  23.2 46.3 %all-to-all-done.column = f32[32,128,128]{2,1,0:T(8,128)S(1)} async-done(((f32[32,128,128]{2,1,0:T(8,128)}), f32[32,128,128]{2,1,0:T(8,128)S(1)}, u32[]{:S(2)}, u32[]{:S(2)}) %all-to-all-start) | async-done | bytes 2097184 | tf_op jit(solution)/shard_map/all_to_all | solution.py:639
  69.5 0.0 copy-start
  69.5 1.3 copy-done
  70.8 14.5 %column_filter.1 = f32[32,80,128]{2,1,0:T(8,128)} custom-call(f32[2]{0:T(128)} %pad_maximum_fusion.1.scale, f32[32,128,128]{2,1,0:T(8,128)} %copy-done, f32[128,128]{1,0:T(8,128)} %constant.104.clone.table, f32[256,256]{1,0:T(8,128)} %constant.105.clone.forward_w.inverse_w, f32[256,256]{1,0:T(8,128)} %constant.106.clone.special_f, ...), custom_call_target="tpu_custom_call" | custom-call | tf_op jit(solution)/shard_map/column_filter/pallas_call | solution.py:267
  85.3 0.0 copy-start.2
  85.3 0.0 copy-start.3
  85.3 4.1 %all-to-all-start.1 = ((f32[32,80,128]{2,1,0:T(8,128)}), f32[32,80,128]{2,1,0:T(8,128)S(1)}, u32[]{:S(2)}, u32[]{:S(2)}) async-start(f32[32,80,128]{2,1,0:T(8,128)} %column_filter.1), calls=%async_computation.1 | async-start | bytes 2621440 | tf_op jit(solution)/shard_map/all_to_all | solution.py:639
  89.4 0.0 copy-done.2
  89.4 2.2 %collective-permute-start = (f32[8,2048]{1,0:T(8,128)S(1)}, f32[8,2048]{1,0:T(8,128)S(1)}, u32[]{:S(2)}, u32[]{:S(2)}) collective-permute-start(f32[8,2048]{1,0:T(8,128)S(1)} %get-tuple-element.17), channel_id=1, source_target_pairs={{0,1},{1,2},{2,3},{3,4},{4,5},{5,6},{6,7},{7,8},{8,9},{9,10},{10,1... | collective-permute-start | bytes 196616 | tf_op jit(solution)/shard_map/ppermute | solution.py:660
  91.6 1.5 %collective-permute-start.1 = (f32[8,2048]{1,0:T(8,128)S(1)}, f32[8,2048]{1,0:T(8,128)S(1)}, u32[]{:S(2)}, u32[]{:S(2)}) collective-permute-start(f32[8,2048]{1,0:T(8,128)S(1)} %get-tuple-element.18), channel_id=1, source_target_pairs={{1,0},{2,1},{3,2},{4,3},{5,4},{6,5},{7,6},{8,7},{9,8},{10,9},{11,1... | collective-permute-start | bytes 196616 | tf_op jit(solution)/shard_map/ppermute | solution.py:661
  93.1 0.0 copy-done.3
  93.1 0.6 add_select_fusion
  93.7 5.9 %observe.1 = (f32[64,2048]{1,0:T(8,128)}, f32[64,2048]{1,0:T(8,128)}) custom-call(s32[1,2048]{1,0:T(1,128)} %bitcast.10, s32[1,2048]{1,0:T(1,128)} %bitcast.9, f32[1,2048]{1,0:T(1,128)} %bitcast.7), custom_call_target="tpu_custom_call" | custom-call | flops 2147483648 | bytes 1048576 | tf_op jit(solution)/shard_map/observe/pallas_call | solution.py:311
  99.6 0.7 pad_add_fusion.origin
  100.3 0.0 collective-permute-done
  100.3 0.0 collective-permute-done.1
  100.3 0.9 pad_maximum_fusion.source
  101.2 20.2 %all-to-all-done.1.coefs = f32[32,80,128]{2,1,0:T(8,128)S(1)} async-done(((f32[32,80,128]{2,1,0:T(8,128)}), f32[32,80,128]{2,1,0:T(8,128)S(1)}, u32[]{:S(2)}, u32[]{:S(2)}) %all-to-all-start.1) | async-done | bytes 1310752 | tf_op jit(solution)/shard_map/all_to_all | solution.py:639
  121.3 0.0 copy-start.1
  121.3 1.1 copy-done.1
  122.4 10.0 %krylov.1 = (f32[64,2048]{1,0:T(8,128)}, f32[4,64,2048]{2,1,0:T(8,128)}, f32[32,1,128]{2,1,0:T(1,128)}) custom-call(s32[2]{0:T(128)} %pad_add_fusion.origin, f32[32,80,128]{2,1,0:T(8,128)} %copy-done.1, f32[80,2048]{1,0:T(8,128)} %pad_maximum_fusion.source, f32[64,2048]{1,0:T(8,128)} %get-tuple-element.10.count, f32[64,2048]{1,0:T(8,128)} %get-tuple-element.11.total, ...), custom_call_target="tpu_custom_call" | custom-call | tf_op jit(solution)/shard_map/krylov/pallas_call | solution.py:534
  132.3 11.4 %all_to_all.15.partial = f32[32,1,128]{2,1,0:T(1,128)} all-to-all(f32[32,1,128]{2,1,0:T(1,128)} %get-tuple-element.13), channel_id=1, replica_groups=mesh['strip'=32] {'strip'}, dimensions={0} | all-to-all | bytes 32768 | tf_op jit(solution)/shard_map/all_to_all | solution.py:639
  143.8 3.2 %finish.1 = (f32[64,2048]{1,0:T(8,128)}, f32[1,128]{1,0:T(1,128)}) custom-call(f32[32,1,128]{2,1,0:T(1,128)} %all_to_all.15.partial, f32[4,64,2048]{2,1,0:T(8,128)} %get-tuple-element.14.basis, f32[16,128]{1,0:T(8,128)} %bitcast.8), custom_call_target="tpu_custom_call" | custom-call | tf_op jit(solution)/shard_map/finish/pallas_call | solution.py:626
  (1 shorter events, 0.0 us)
Async XLA Ops:
  13.4 56.1 %all-to-all-start = ((f32[32,128,128]{2,1,0:T(8,128)}), f32[32,128,128]{2,1,0:T(8,128)S(1)}, u32[]{:S(2)}, u32[]{:S(2)}) async-start(f32[32,128,128]{2,1,0:T(8,128)} %row_forward.1), calls=%async_computation | async-start | bytes 4194304 | tf_op jit(solution)/shard_map/all_to_all | solution.py:639
  69.5 1.3 copy-start
  85.3 4.1 %copy-start.2 = (f32[64,2048]{1,0:T(8,128)S(1)}, f32[64,2048]{1,0:T(8,128)}, u32[]{:S(2)}) copy-start(f32[64,2048]{1,0:T(8,128)} %param.23) | copy-start | bytes 1572868
  85.3 7.8 %copy-start.3 = (s32[2048]{0:T(1024)S(1)}, s32[2048]{0:T(1024)}, u32[]{:S(2)}) copy-start(s32[2048]{0:T(1024)} %param.24) | copy-start | bytes 24580
  85.3 36.0 %all-to-all-start.1 = ((f32[32,80,128]{2,1,0:T(8,128)}), f32[32,80,128]{2,1,0:T(8,128)S(1)}, u32[]{:S(2)}, u32[]{:S(2)}) async-start(f32[32,80,128]{2,1,0:T(8,128)} %column_filter.1), calls=%async_computation.1 | async-start | bytes 2621440 | tf_op jit(solution)/shard_map/all_to_all | solution.py:639
  89.4 10.9 %collective-permute-start = (f32[8,2048]{1,0:T(8,128)S(1)}, f32[8,2048]{1,0:T(8,128)S(1)}, u32[]{:S(2)}, u32[]{:S(2)}) collective-permute-start(f32[8,2048]{1,0:T(8,128)S(1)} %get-tuple-element.17), channel_id=1, source_target_pairs={{0,1},{1,2},{2,3},{3,4},{4,5},{5,6},{6,7},{7,8},{8,9},{9,10},{10,1... | collective-permute-start | bytes 196616 | tf_op jit(solution)/shard_map/ppermute | solution.py:660
  91.6 8.7 %collective-permute-start.1 = (f32[8,2048]{1,0:T(8,128)S(1)}, f32[8,2048]{1,0:T(8,128)S(1)}, u32[]{:S(2)}, u32[]{:S(2)}) collective-permute-start(f32[8,2048]{1,0:T(8,128)S(1)} %get-tuple-element.18), channel_id=1, source_target_pairs={{1,0},{2,1},{3,2},{4,3},{5,4},{6,5},{7,6},{8,7},{9,8},{10,9},{11,1... | collective-permute-start | bytes 196616 | tf_op jit(solution)/shard_map/ppermute | solution.py:661
  121.3 1.1 copy-start.1

commit v2 on v1

--- a/solution.py
+++ b/solution.py
@@ -12,19 +12,51 @@
 ITERS = 4
 LANES = 128
 HALO = 8
+ABOVE = ITERS
+BELOW = ITERS + 1
 TERMS = 2 * ITERS
 PAIRS = [(i, j) for i in range(ITERS) for j in range(i, ITERS)]
 SUMS = TERMS + len(PAIRS) + ITERS
 
 
-def mm(left, right):
+def dot(left, right):
     return lax.dot_general(
-        left,
-        right,
-        (((1,), (0,)), ((), ())),
-        precision=lax.Precision.HIGHEST,
-        preferred_element_type=jnp.float32,
+        left, right, (((1,), (0,)), ((), ())), preferred_element_type=jnp.float32
     )
+
+
+def halves(value):
+    high = value.astype(jnp.bfloat16)
+    return high, (value - high.astype(jnp.float32)).astype(jnp.bfloat16)
+
+
+def rows_times(value, table):
+    size = value.shape[1]
+    high, low = halves(value)
+    upper = table[:size, :]
+    return dot(high, table[size:, :]) + dot(low, upper) + dot(high, upper)
+
+
+def times_columns(table, value):
+    size = value.shape[0]
+    high, low = halves(value)
+    upper = table[:size, :]
+    return dot(table[size:, :], high) + dot(upper, low) + dot(upper, high)
+
+
+def pieces(table):
+    table = np.asarray(table, np.float64)
+    high = table.astype(jnp.bfloat16)
+    low = (table - high.astype(np.float64)).astype(jnp.bfloat16)
+    return np.concatenate([high, low], 0)
+
+
+def near(value):
+    return pltpu.with_memory_space_constraint(value, pltpu.VMEM)
+
+
+def far(value):
+    return pltpu.with_memory_space_constraint(value, pltpu.HBM)
 
 
 def dft_tables():
@@ -153,14 +185,17 @@
             work[j, pl.ds(base, 8), LANES:] = im * c - re * s
         return carry
 
-    lax.fori_loop(0, rows // 8, group, 0)
-    first = mm(work[0], special_w[...])
-    out[0] = first[:, :LANES]
-    out[1] = first[:, LANES:]
-    for j in range(1, half):
-        value = mm(work[j], pair_w[...])
-        out[2 * j] = value[:, :LANES]
-        out[2 * j + 1] = value[:, LANES:]
+    lax.fori_loop(0, rows // 8, group, 0, unroll=4)
+    put = slice(None)
+    first = rows_times(work[0], special_w)
+    out[0, put, :] = first[:, :LANES]
+    out[1, put, :] = first[:, LANES:]
+    batch = 5
+    for begin in range(1, half, batch):
+        value = rows_times(work[begin : begin + batch].reshape(batch * rows, 2 * LANES), pair_w)
+        for k in range(batch):
+            out[2 * (begin + k), put, :] = value[k * rows : (k + 1) * rows, :LANES]
+            out[2 * (begin + k) + 1, put, :] = value[k * rows : (k + 1) * rows, LANES:]
 
 
 def row_forward(state, noise, step, tables):
@@ -181,10 +216,11 @@
             pl.BlockSpec(special_w.shape, whole),
         ],
         out_specs=pl.BlockSpec((factor, block, LANES), lambda i: (0, i, 0)),
-        out_shape=jax.ShapeDtypeStruct((factor, rows, LANES), jnp.float32),
+        out_shape=pltpu.HBM((factor, rows, LANES), jnp.float32),
         scratch_shapes=[pltpu.VMEM((factor // 2, block, 2 * LANES), jnp.float32)],
+        compiler_params=pltpu.CompilerParams(vmem_limit_bytes=16 << 20),
         name="row_forward",
-    )(step, state, noise, twiddle, pair_w, special_w)
+    )(step, far(state), far(noise), far(twiddle), far(pair_w), far(special_w))
 
 
 def column_kernel(
@@ -193,7 +229,7 @@
     factor, _, width = column.shape
     half = factor // 2
     length = factor * LANES
-    parts = out.shape[0]
+    extent = field_rows + ABOVE + BELOW
 
     def ahead(index, carry):
         base = pl.multiple_of(index * 8, 8)
@@ -211,7 +247,7 @@
             work[j, high, :] = im * c - re * s
         return carry
 
-    lax.fori_loop(0, LANES // 8, ahead, 0)
+    lax.fori_loop(0, LANES // 8, ahead, 0, unroll=4)
     place = lax.broadcasted_iota(jnp.int32, (LANES, width), 0)
     side = wave[...] + scale[1]
     gain = scale[0]
@@ -220,19 +256,25 @@
         freq = jnp.minimum(freq, length - freq).astype(jnp.float32)
         return gain / (freq * freq + side)
 
+    batch = 2 if width % LANES == 0 else 1
     for j in range(half):
         if j == 0:
-            value = mm(special_f[...], work[0])
-            halves = LANES // 2
-            top = amplitude(factor * jnp.where(place > halves, place - halves, place))
-            low = amplitude(half + factor * jnp.where(place >= halves, place - halves, place))
+            value = times_columns(special_f, work[0])
+            middle = LANES // 2
+            top = amplitude(factor * jnp.where(place > middle, place - middle, place))
+            low = amplitude(half + factor * jnp.where(place >= middle, place - middle, place))
             value = jnp.concatenate([value[:LANES] * top, value[LANES:] * low], axis=0)
-            work[0] = mm(special_i[...], value)
-        else:
-            value = mm(forward_w[...], work[j])
-            top = amplitude(j + factor * place)
-            value = jnp.concatenate([value[:LANES] * top, value[LANES:] * top], axis=0)
-            work[j] = mm(inverse_w[...], value)
+            work[0] = times_columns(special_i, value)
+            continue
+        if (j - 1) % batch:
+            continue
+        block = range(j, min(j + batch, half))
+        value = times_columns(forward_w, jnp.concatenate([work[k] for k in block], axis=1))
+        top = jnp.concatenate([amplitude(k + factor * place) for k in block], axis=1)
+        value = jnp.concatenate([value[:LANES] * top, value[LANES:] * top], axis=0)
+        value = times_columns(inverse_w, value)
+        for k in block:
+            work[k] = value[:, (k - j) * width : (k - j + 1) * width]
 
     rim = jnp.zeros((HALO, width), jnp.float32)
     field[:HALO, :] = rim
@@ -255,9 +297,10 @@
             field[pl.ds(pl.multiple_of(base + HALO + LANES * a, 8), 8), :] = values[a]
         return carry
 
-    lax.fori_loop(0, LANES // 8, back, 0)
-    for part in range(parts):
-        out[part] = field[field_rows * part : field_rows * (part + 1) + 2 * HALO, :]
+    lax.fori_loop(0, LANES // 8, back, 0, unroll=4)
+    for part in range(out.shape[0] // extent):
+        begin = HALO - ABOVE + field_rows * part
+        out[extent * part : extent * (part + 1), :] = field[begin : begin + extent, :]
 
 
 def column_filter(column, scale, wave, tables, parts, field_rows):
@@ -268,13 +311,14 @@
         functools.partial(column_kernel, field_rows=field_rows),
         in_specs=[pl.BlockSpec(memory_space=pltpu.SMEM)] + [vmem] * 7,
         out_specs=vmem,
-        out_shape=jax.ShapeDtypeStruct((parts, field_rows + 2 * HALO, width), jnp.float32),
+        out_shape=pltpu.HBM((parts * (field_rows + ABOVE + BELOW), width), jnp.float32),
         scratch_shapes=[
             pltpu.VMEM((factor // 2, 2 * LANES, width), jnp.float32),
             pltpu.VMEM((length // 2 + 2 * HALO, width), jnp.float32),
         ],
+        compiler_params=pltpu.CompilerParams(vmem_limit_bytes=24 << 20),
         name="column_filter",
-    )(scale, column, *tables, wave)
+    )(scale, near(column), *tables, wave)
 
 
 def observe_kernel(local, cells, values, count, total, left):
@@ -310,6 +354,7 @@
     shape = jax.ShapeDtypeStruct((rows, columns), jnp.float32)
     return pl.pallas_call(
         observe_kernel,
+        compiler_params=pltpu.CompilerParams(vmem_limit_bytes=32 << 20),
         grid=(columns // block,),
         in_specs=[whole, whole, whole],
         out_specs=(piece, piece),
@@ -374,36 +419,68 @@
     return other, (low + pltpu.roll(low, shift, axis)) + error
 
 
-def tile_sum(value):
-    pieces = [value[:, LANES * i : LANES * (i + 1)] for i in range(value.shape[1] // LANES)]
+def fold_rows(value):
+    pieces = [value[8 * i : 8 * i + 8] for i in range(value.shape[0] // 8)]
     while len(pieces) > 1:
-        pieces = [a + b for a, b in zip(pieces[0::2], pieces[1::2])]
+        last = [pieces[-1]] if len(pieces) % 2 else []
+        pieces = [a + b for a, b in zip(pieces[0::2], pieces[1::2])] + last
     return pieces[0]
 
 
 def krylov_kernel(
-    origin, coefs, source, count, total, twiddle, inverse_w, special_i,
-    log_perm, basis, partial,
-    work, kappa, centre, inverse, north, south, west, east, vector,
+    origin, coefs, source_hbm, count_hbm, total_hbm, twiddle, inverse_w, special_i,
+    log_perm_hbm, basis, partial,
+    received, work, kappa, centre, inverse, north, west, east, vector,
+    source, count, total, log_perm, arrive, leave,
 ):
-    factor, extent, _ = coefs.shape
-    half = factor // 2
-    columns = half * LANES
-    rows = extent - 2 * HALO
-    groups = extent // 8
-    pair = jnp.concatenate([coefs[0], coefs[1]], axis=1)
-    work[0] = mm(pair, special_i[...])
-    for j in range(1, half):
-        pair = jnp.concatenate([coefs[2 * j], coefs[2 * j + 1]], axis=1)
-        work[j] = mm(pair, inverse_w[...])
-
-    rim = jnp.zeros((8, columns), jnp.float32)
-    for ref in (kappa, vector.at[0], vector.at[1]):
-        ref[:8, :] = rim
-        ref[8 + extent :, :] = rim
+    inward = [
+        pltpu.make_async_copy(far_ref, near_ref, arrive.at[k])
+        for k, (far_ref, near_ref) in enumerate(
+            ((source_hbm, source), (count_hbm, count), (total_hbm, total))
+        )
+    ]
+    outward = pltpu.make_async_copy(log_perm, log_perm_hbm, leave)
+    for copy in inward:
+        copy.start()
+    half, area, _ = work.shape
+    factor = 2 * half
+    rows = area - 2 * HALO
+    extent = rows + ABOVE + BELOW
+    groups = area // 8
+
+    size = coefs.shape[0]
+    rim = jnp.zeros((8, LANES), jnp.float32)
+    received[:8, :] = rim
+    received[8 + size : 16 + size, :] = rim
+    received[8 : 8 + size, :] = coefs[...]
+
+    def window(tile):
+        begin = 8 + extent * tile + ABOVE - HALO
+        return received[begin : begin + area, :]
+
+    def pair(j):
+        return jnp.concatenate([window(2 * j), window(2 * j + 1)], axis=1)
+
+    work[0] = rows_times(pair(0), special_i)
+    batch = 3
+    for j in range(1, half, batch):
+        value = rows_times(jnp.concatenate([pair(k) for k in range(j, j + batch)], axis=0), inverse_w)
+        for k in range(batch):
+            work[j + k] = value[k * area : (k + 1) * area]
+
+    for tile in range(half):
+        for ref in (kappa, vector.at[0], vector.at[1]):
+            ref[tile, :8, :] = rim
+            ref[tile, 8 + area :, :] = rim
 
     first_row = origin[0] - HALO
     limit = origin[1]
+
+    def usable(start, count):
+        local = lax.broadcasted_iota(jnp.int32, (count, LANES), 0) + start
+        row = local + first_row
+        inner = (local >= HALO - ABOVE) & (local < HALO + rows + BELOW)
+        return inner & (row >= 0) & (row < limit)
 
     def inverse_group(index, carry):
         base = pl.multiple_of(index * 8, 8)
@@ -416,11 +493,10 @@
             spectrum.append((re * c - im * s, re * s + im * c))
         spectrum.append((work[0, low, LANES:], None))
         values = irfft(spectrum, factor)
-        row = lax.broadcasted_iota(jnp.int32, (8, LANES), 0) + (base + first_row)
-        valid = (row >= 0) & (row < limit)
+        valid = usable(base, 8)
         store = pl.ds(pl.multiple_of(base + 8, 8), 8)
         for a in range(half):
-            kappa[store, LANES * a : LANES * (a + 1)] = jnp.where(valid, jnp.exp(values[a]), 0.0)
+            kappa[a, store, :] = jnp.where(valid, 0.5 * jnp.exp(values[a]), 0.0)
 
         @pl.when((index >= HALO // 8) & (index < groups - HALO // 8))
         def _():
@@ -430,86 +506,106 @@
 
         return carry
 
-    lax.fori_loop(0, groups, inverse_group, 0)
-
-    lane = lax.broadcasted_iota(jnp.int32, (8, columns), 1)
-    inner_west = lane > 0
-    inner_east = lane < columns - 1
-    zero = jnp.zeros((8, LANES), jnp.float32)
-    sums = [zero] * SUMS
-
-    for group in range(groups):
-        at = 8 + 8 * group
-        own = HALO // 8 <= group < groups - HALO // 8
-        here = kappa[at : at + 8, :]
-        up = 0.5 * (here + kappa[at - 1 : at + 7, :])
-        down = 0.5 * (here + kappa[at + 1 : at + 9, :])
-        left = jnp.where(inner_west, pltpu.roll(here, 1, 1), 0.0)
-        right = jnp.where(inner_east, pltpu.roll(here, columns - 1, 1), 0.0)
-        left = 0.5 * (here + left)
-        right = 0.5 * (here + right)
+    lax.fori_loop(0, groups, inverse_group, 0, unroll=2)
+    outward.start()
+    inward[0].wait()
+
+    first_lane = lax.broadcasted_iota(jnp.int32, (1, LANES), 1) == 0
+    last_lane = lax.broadcasted_iota(jnp.int32, (1, LANES), 1) == LANES - 1
+    sums = [rim] * SUMS
+    own = slice(HALO, HALO + rows)
+    every = slice(8, 8 + area)
+    before = slice(7, 7 + area)
+    after = slice(9, 9 + area)
+
+    def sideways(load):
+        back, ahead = None, None
+        value = load(0)
+        for tile in range(half):
+            following = load(tile + 1) if tile + 1 < half else None
+            turned = pltpu.roll(value, 1, 1)
+            ahead = pltpu.roll(value, LANES - 1, 1) if tile == 0 else ahead
+            left = jnp.where(first_lane, 0.0 if back is None else back, turned)
+            if following is None:
+                right = jnp.where(last_lane, 0.0, ahead)
+            else:
+                next_ahead = pltpu.roll(following, LANES - 1, 1)
+                right = jnp.where(last_lane, next_ahead, ahead)
+                ahead = next_ahead
+            yield tile, value, left, right
+            back, value = turned, following
+
+    valid = usable(0, area)
+    for tile, here, left, right in sideways(lambda t: kappa[t, every, :]):
+        lanes = slice(LANES * tile, LANES * (tile + 1))
+        up = here + kappa[tile, before, :]
+        down = here + kappa[tile, after, :]
+        left = here + left
+        right = here + right
         middle = up + down + left + right
-        row = lax.broadcasted_iota(jnp.int32, (8, columns), 0) + (8 * group + first_row)
-        rest = jnp.where((row >= 0) & (row < limit), 1.0 / middle, 0.0)
-        put = slice(8 * group, 8 * group + 8)
-        centre[put, :] = middle
-        inverse[put, :] = rest
-        north[put, :] = up
-        south[put, :] = down
-        west[put, :] = jnp.where(inner_west, left, 0.0)
-        east[put, :] = jnp.where(inner_east, right, 0.0)
-        first = source[put, :]
+        rest = jnp.where(valid, 1.0 / middle, 0.0)
+        centre[tile] = middle
+        inverse[tile] = rest
+        north[tile, :area, :] = up
+        north[tile, area:, :] = rim
+        west[tile] = left
+        east[tile] = right
+        first = source[:, lanes]
         value = first * rest
-        vector[0, at : at + 8, :] = value
-        if own:
-            basis[0, 8 * group - HALO : 8 * group - HALO + 8, :] = value
-            sums[0] = sums[0] + tile_sum(first * value)
-
-    for step in range(ITERS):
+        vector[0, tile, every, :] = value
+        basis[0, :, lanes] = value[own]
+        sums[0] = sums[0] + fold_rows((first * value)[own])
+
+    for step in range(ITERS - 1):
         now = vector.at[step % 2]
         new = vector.at[(step + 1) % 2]
-        for group in range(groups):
-            at = 8 + 8 * group
-            own = HALO // 8 <= group < groups - HALO // 8
-            if step == ITERS - 1 and not own:
-                continue
-            put = slice(8 * group, 8 * group + 8)
-            here = now[at : at + 8, :]
+        for tile, here, left, right in sideways(lambda t: now[t, every, :]):
             image = (
-                centre[put, :] * here
-                - north[put, :] * now[at - 1 : at + 7, :]
-                - south[put, :] * now[at + 1 : at + 9, :]
-                - west[put, :] * pltpu.roll(here, 1, 1)
-                - east[put, :] * pltpu.roll(here, columns - 1, 1)
+                centre[tile] * here
+                - north[tile, :area, :] * now[tile, before, :]
+                - north[tile, 1 : area + 1, :] * now[tile, after, :]
+                - west[tile] * left
+                - east[tile] * right
             )
-            if own:
-                sums[2 * step + 1] = sums[2 * step + 1] + tile_sum(here * image)
-            if step < ITERS - 1:
-                value = image * inverse[put, :]
-                new[at : at + 8, :] = value
-                if own:
-                    basis[step + 1, 8 * group - HALO : 8 * group - HALO + 8, :] = value
-                    sums[2 * step + 2] = sums[2 * step + 2] + tile_sum(value * image)
-
-    for group in range(rows // 8):
-        put = slice(8 * group, 8 * group + 8)
-        vectors = [basis[k, put, :] for k in range(ITERS)]
-        weight = count[put, :]
+            value = image * inverse[tile]
+            new[tile, every, :] = value
+            basis[step + 1, :, LANES * tile : LANES * (tile + 1)] = value[own]
+            sums[2 * step + 1] = sums[2 * step + 1] + fold_rows((here * image)[own])
+            sums[2 * step + 2] = sums[2 * step + 2] + fold_rows((value * image)[own])
+
+    inward[1].wait()
+    inward[2].wait()
+    now = vector.at[(ITERS - 1) % 2]
+    back = None
+    for tile in range(half):
+        lanes = slice(LANES * tile, LANES * (tile + 1))
+        here = now[tile, 8 + HALO : 8 + HALO + rows, :]
+        turned = pltpu.roll(here, 1, 1)
+        left = jnp.where(first_lane, 0.0 if back is None else back, turned)
+        back = turned
+        shared = (
+            north[tile, HALO + 1 : HALO + 1 + rows, :] * now[tile, 9 + HALO : 9 + HALO + rows, :]
+            + west[tile, own, :] * left
+        )
+        energy = here * (centre[tile, own, :] * here - 2.0 * shared)
+        sums[TERMS - 1] = sums[TERMS - 1] + fold_rows(energy)
+        vectors = [basis[k, :, lanes] for k in range(ITERS)]
+        weight = count[:, lanes]
         weighted = [weight * v for v in vectors]
         for spot, (i, j) in enumerate(PAIRS):
-            sums[TERMS + spot] = sums[TERMS + spot] + tile_sum(weighted[i] * vectors[j])
-        datum = total[put, :]
+            sums[TERMS + spot] = sums[TERMS + spot] + fold_rows(weighted[i] * vectors[j])
+        datum = total[:, lanes]
         for k in range(ITERS):
             slot = TERMS + len(PAIRS) + k
-            sums[slot] = sums[slot] + tile_sum(datum * vectors[k])
+            sums[slot] = sums[slot] + fold_rows(datum * vectors[k])
 
     sub = lax.broadcasted_iota(jnp.int32, (8, LANES), 0)
     spot = lax.broadcasted_iota(jnp.int32, (8, LANES), 1)
-    row = zero
+    row = rim
     for begin in range(0, SUMS, 8):
-        high, low = zero, zero
+        high, low = rim, rim
         for k in range(begin, min(begin + 8, SUMS)):
-            h, e = sums[k], zero
+            h, e = sums[k], rim
             for shift in (4, 2, 1):
                 h, e = fold(h, e, shift, 0)
             high = jnp.where(sub == k - begin, h, high)
@@ -522,37 +618,47 @@
         row = row + pltpu.roll(row, shift, 0)
     for part in range(partial.shape[0]):
         partial[part] = row[:1]
+    outward.wait()
 
 
 def krylov(origin, coefs, source, count, total, tables, parts):
-    factor, extent, _ = coefs.shape
-    columns = factor // 2 * LANES
-    rows = extent - 2 * HALO
+    area, columns = source.shape
+    half = columns // LANES
+    rows = area - 2 * HALO
     vmem = pl.BlockSpec(memory_space=pltpu.VMEM)
-    plane = pltpu.VMEM((extent, columns), jnp.float32)
-    padded = pltpu.VMEM((extent + 16, columns), jnp.float32)
+    anywhere = pl.BlockSpec(memory_space=pl.ANY)
+    plane = pltpu.VMEM((half, area, LANES), jnp.float32)
+    padded = pltpu.VMEM((half, area + 16, LANES), jnp.float32)
+    strip = pltpu.VMEM((rows, columns), jnp.float32)
     return pl.pallas_call(
         krylov_kernel,
-        in_specs=[pl.BlockSpec(memory_space=pltpu.SMEM)] + [vmem] * 7,
-        out_specs=(vmem, vmem, vmem),
+        in_specs=[pl.BlockSpec(memory_space=pltpu.SMEM), vmem] + [anywhere] * 3 + [vmem] * 3,
+        out_specs=(anywhere, vmem, vmem),
         out_shape=(
-            jax.ShapeDtypeStruct((rows, columns), jnp.float32),
-            jax.ShapeDtypeStruct((ITERS, rows, columns), jnp.float32),
-            jax.ShapeDtypeStruct((parts, 1, LANES), jnp.float32),
+            pltpu.HBM((rows, columns), jnp.float32),
+            pltpu.VMEM((ITERS, rows, columns), jnp.float32),
+            pltpu.VMEM((parts, 1, LANES), jnp.float32),
         ),
         scratch_shapes=[
-            pltpu.VMEM((factor // 2, extent, 2 * LANES), jnp.float32),
+            pltpu.VMEM((coefs.shape[0] + 16, LANES), jnp.float32),
+            pltpu.VMEM((half, area, 2 * LANES), jnp.float32),
             padded,
             plane,
             plane,
+            pltpu.VMEM((half, area + 8, LANES), jnp.float32),
             plane,
             plane,
-            plane,
-            plane,
-            pltpu.VMEM((2, extent + 16, columns), jnp.float32),
+            pltpu.VMEM((2, half, area + 16, LANES), jnp.float32),
+            pltpu.VMEM((area, columns), jnp.float32),
+            strip,
+            strip,
+            strip,
+            pltpu.SemaphoreType.DMA((3,)),
+            pltpu.SemaphoreType.DMA(()),
         ],
+        compiler_params=pltpu.CompilerParams(vmem_limit_bytes=32 << 20),
         name="krylov",
-    )(origin, coefs, source, count, total, *tables)
+    )(origin, near(coefs), far(source), far(count), far(total), *tables)
 
 
 def final_kernel(partial, basis, values, pressure, loglik):
@@ -631,8 +737,9 @@
             jax.ShapeDtypeStruct(basis.shape[1:], jnp.float32),
             jax.ShapeDtypeStruct((1, LANES), jnp.float32),
         ),
+        compiler_params=pltpu.CompilerParams(vmem_limit_bytes=16 << 20),
         name="finish",
-    )(partial, basis, values)
+    )(near(partial), near(basis), near(values))
 
 
 def exchange(block):
@@ -649,7 +756,7 @@
     ways = parts // factor
     field_rows, columns = source.shape
 
-    forward, inverse, special_f, special_i = (np.float32(t) for t in dft_tables())
+    forward, inverse, special_f, special_i = dft_tables()
     cos, sin = twiddle_table(length, factor)
     across = np.float32(np.concatenate([cos, sin], 0))
     down = np.zeros((LANES, LANES), np.float32)
@@ -666,7 +773,7 @@
         cell_row[None, :], (obs_cells % columns)[None, :], obs_values[None, :], field_rows, columns
     )
 
-    tiles = row_forward(state, noise, step, (across, forward, special_f))
+    tiles = row_forward(state, noise, step, (across, pieces(forward), pieces(special_f)))
     if ways > 1:
         tiles = tiles.reshape(factor, rows_here, ways, width).transpose(0, 2, 1, 3)
         tiles = tiles.reshape(parts, rows_here, width)
@@ -692,19 +799,19 @@
         column,
         scale,
         freq * freq,
-        (down, forward.T, special_f.T, inverse.T, special_i.T),
+        (down, *(pieces(t.T) for t in (forward, special_f, inverse, special_i))),
         parts,
         field_rows,
     )
-    coefs = exchange(blocks)
-    extent = field_rows + 2 * HALO
+    extent = field_rows + ABOVE + BELOW
+    coefs = exchange(blocks.reshape(parts, 1, extent * width))
     if ways > 1:
         coefs = coefs.reshape(factor, ways, extent, width).transpose(0, 2, 1, 3)
-        coefs = coefs.reshape(factor, extent, LANES)
+    coefs = coefs.reshape(factor * extent, LANES)
 
     origin = jnp.stack([position * field_rows, parts * field_rows]).astype(jnp.int32)
     log_perm, basis, partial = krylov(
-        origin, coefs, wide_source, count, total, (across, inverse, special_i), parts
+        origin, coefs, wide_source, count, total, (across, pieces(inverse), pieces(special_i)), parts
     )
     pressure, loglik = finish(exchange(partial), basis, obs_values.reshape(-1, LANES))
     return (log_perm, pressure, loglik[0, 0])

time: 147 us -> 122 us (0.83)
  Pallas kernels: 45.7 us -> 23 us
  other arithmetic: 3.28 us -> 1.13 us
  local copies, waits for them, and re-layouts: 2.42 us -> 0.85 us
    pallas_call x1, Pallas kernels: 14.5 us -> 6.68 us  [column_filter(): pl.pallas_call(functools.partial(column_kernel, field_rows=field_rows), i...]
    pallas_call x1, Pallas kernels: 12.1 us -> 5.41 us  [row_forward(): pl.pallas_call(functools.partial(row_kernel, factor=factor), grid=(rows /...]
    pallas_call x1, Pallas kernels: 9.95 us -> 5.17 us  [krylov(): pl.pallas_call(krylov_kernel, in_specs=[pl.BlockSpec(memory_space=pltpu.S...]
    pallas_call x1, Pallas kernels: 5.93 us -> 4.17 us  [observe(): pl.pallas_call(observe_kernel, compiler_params=pltpu.CompilerParams(vmem_...]
    pallas_call x1, Pallas kernels: 3.18 us -> 1.6 us  [finish(): pl.pallas_call(final_kernel, in_specs=[vmem] * 3, out_specs=(vmem, vmem),...]
    unnamed x8 -> x24, local copies, waits for them, and re-layouts: 2.4 us -> 0.84 us
  transfers between devices with their start and end apart: 4 -> 4, of which waited for: 2 -> 2; matrix products, arithmetic and copies ran while one was open for 2% -> 1% of each run, Pallas kernels for 4% -> 3%
where the time goes in v2:
time: 122 us; the launch traced here: 121 us
  waiting for transfers between devices  67.1 us (55%)
  Pallas kernels  23 us (19%)
  starting transfers between devices  14.9 us (12%)
  blocking collectives  11.3 us (9%)
  between operations  2.75 us (2%)
    all_to_all x2, waiting for transfers between devices, exchange(): lax.all_to_all(block, 'strip', split_axis=0, concat_axis=0, tiled=True)  67.1 us
    all_to_all x2, starting transfers between devices, exchange(): lax.all_to_all(block, 'strip', split_axis=0, concat_axis=0, tiled=True)  11.4 us
    all_to_all x1, blocking collectives, exchange(): lax.all_to_all(block, 'strip', split_axis=0, concat_axis=0, tiled=True)  11.3 us
    pallas_call x1, Pallas kernels, column_filter(): pl.pallas_call(functools.partial(column_kernel, field_rows=field_rows), i...  6.68 us
    pallas_call x1, Pallas kernels, row_forward(): pl.pallas_call(functools.partial(row_kernel, factor=factor), grid=(rows /...  5.41 us
    pallas_call x1, Pallas kernels, krylov(): pl.pallas_call(krylov_kernel, in_specs=[pl.BlockSpec(memory_space=pltpu.S...  5.17 us
    pallas_call x1, Pallas kernels, observe(): pl.pallas_call(observe_kernel, compiler_params=pltpu.CompilerParams(vmem_...  4.17 us
  transfers between devices with their start and end apart: 4, of which 2 were waited for; matrix products, arithmetic and copies ran while one was open for 1% of the time, Pallas kernels for 3%

profile of v2, /device:TPU:0, one launch (start us, length us, event | category | flops | bytes accessed | tf_op | source)
XLA Modules:
  0.0 121.1 jit_solution(153351636937892540)
XLA Ops:
  1.3 5.4 %row_forward.1 = f32[32,128,128]{2,1,0:T(8,128)} custom-call(f32[1]{0:T(128)S(6)} %copy.22.step, f32[128,4096]{1,0:T(8,128)} %state.1, f32[128,4096]{1,0:T(8,128)} %noise.1, f32[32,128]{1,0:T(8,128)} %constant.101.clone.twiddle, bf16[512,256]{1,0:T(8,128)(2,1)} %constant.102.clone.pair_w.inverse_w, bf16[512,256]{1,0:T(8,128)(2,1)} %constant.103.clone.special_w), custom_call_target="tpu_custom_call" | custom-call | tf_op jit(solution)/shard_map/row_forward/pallas_call | solution.py:207
  6.7 0.0 copy-start.6
  6.7 0.0 copy-start.7
  6.7 7.3 %all-to-all-start = ((f32[32,128,128]{2,1,0:T(8,128)}), f32[32,128,128]{2,1,0:T(8,128)S(1)}, u32[]{:S(2)}, u32[]{:S(2)}) async-start(f32[32,128,128]{2,1,0:T(8,128)} %row_forward.1), calls=%async_computation | async-start | bytes 4194304 | tf_op jit(solution)/shard_map/all_to_all | solution.py:746
  15.4 0.1 pad_maximum_fusion.1.scale
  15.5 47.3 %all-to-all-done.column = f32[32,128,128]{2,1,0:T(8,128)S(1)} async-done(((f32[32,128,128]{2,1,0:T(8,128)}), f32[32,128,128]{2,1,0:T(8,128)S(1)}, u32[]{:S(2)}, u32[]{:S(2)}) %all-to-all-start) | async-done | bytes 2097184 | tf_op jit(solution)/shard_map/all_to_all | solution.py:746
  62.8 0.0 copy-done
  62.8 0.0 copy-done.1
  62.8 0.0 copy-done.5
  62.8 0.0 copy-done.6
  62.8 0.0 copy-done.7
  62.8 6.7 %column_filter.1 = f32[2336,128]{1,0:T(8,128)} custom-call(f32[2]{0:T(128)S(1)} %pad_maximum_fusion.1.scale, f32[32,128,128]{2,1,0:T(8,128)S(1)} %all-to-all-done.column, f32[128,128]{1,0:T(8,128)S(1)} %copy-done.7, bf16[512,256]{1,0:T(8,128)(2,1)S(1)} %copy-done, bf16[512,256]{1,0:T(8,128)(2,1)S(1)} %copy-done.5, bf16[512,256]{1,0:T(8,128)(2,1)S(1)} %copy-done.1, ...), custom_call_target="tpu_custom_call" | custom-call | tf_op jit(solution)/shard_map/column_filter/pallas_call | solution.py:310
  69.5 4.1 %all-to-all-start.1 = ((f32[32,1,9344]{2,1,0:T(1,128)}), f32[32,1,9344]{2,1,0:T(1,128)S(1)}, u32[]{:S(2)}, u32[]{:S(2)}) async-start(f32[32,1,9344]{2,1,0:T(1,128)} %bitcast.14), calls=%async_computation.1 | async-start | bytes 2392064 | tf_op jit(solution)/shard_map/all_to_all | solution.py:746
  73.6 0.0 copy-done.10
  73.6 2.2 %collective-permute-start = (f32[8,2048]{1,0:T(8,128)S(1)}, f32[8,2048]{1,0:T(8,128)S(1)}, u32[]{:S(2)}, u32[]{:S(2)}) collective-permute-start(f32[8,2048]{1,0:T(8,128)S(1)} %get-tuple-element.17), channel_id=1, source_target_pairs={{0,1},{1,2},{2,3},{3,4},{4,5},{5,6},{6,7},{7,8},{8,9},{9,10},{10,1... | collective-permute-start | bytes 196616 | tf_op jit(solution)/shard_map/ppermute | solution.py:767
  75.8 1.3 %collective-permute-start.1 = (f32[8,2048]{1,0:T(8,128)S(1)}, f32[8,2048]{1,0:T(8,128)S(1)}, u32[]{:S(2)}, u32[]{:S(2)}) collective-permute-start(f32[8,2048]{1,0:T(8,128)S(1)} %get-tuple-element.18), channel_id=1, source_target_pairs={{1,0},{2,1},{3,2},{4,3},{5,4},{6,5},{7,6},{8,7},{9,8},{10,9},{11,1... | collective-permute-start | bytes 196616 | tf_op jit(solution)/shard_map/ppermute | solution.py:768
  77.1 0.0 copy-done.11
  77.1 0.0 copy-done.9
  77.2 0.0 copy-start.4
  77.2 0.0 copy-start.8
  77.2 4.2 %observe.1 = (f32[64,2048]{1,0:T(8,128)S(1)}, f32[64,2048]{1,0:T(8,128)S(1)}) custom-call(s32[1,2048]{1,0:T(1,128)S(1)} %bitcast.13, s32[1,2048]{1,0:T(1,128)S(1)} %bitcast.12, f32[1,2048]{1,0:T(1,128)S(1)} %bitcast.10), custom_call_target="tpu_custom_call" | custom-call | flops 2147483648 | bytes 1048576 | tf_op jit(solution)/shard_map/observe/pallas_call | solution.py:355
  81.4 0.0 copy-start.2
  81.4 0.8 copy-done.2
  82.2 0.1 pad_add_fusion.origin
  82.2 0.0 collective-permute-done
  82.2 0.0 collective-permute-done.1
  82.2 0.9 pad_maximum_fusion.source_hbm
  83.2 19.8 %all-to-all-done.1 = f32[32,1,9344]{2,1,0:T(1,128)S(1)} async-done(((f32[32,1,9344]{2,1,0:T(1,128)}), f32[32,1,9344]{2,1,0:T(1,128)S(1)}, u32[]{:S(2)}, u32[]{:S(2)}) %all-to-all-start.1) | async-done | bytes 1196064 | tf_op jit(solution)/shard_map/all_to_all | solution.py:746
  103.0 0.0 copy-done.8
  103.0 5.2 %krylov.1 = (f32[64,2048]{1,0:T(8,128)}, f32[4,64,2048]{2,1,0:T(8,128)S(1)}, f32[32,1,128]{2,1,0:T(1,128)S(1)}) custom-call(s32[2]{0:T(128)S(1)} %pad_add_fusion.origin, f32[2336,128]{1,0:T(8,128)S(1)} %bitcast.9, f32[80,2048]{1,0:T(8,128)} %pad_maximum_fusion.source_hbm, f32[64,2048]{1,0:T(8,128)} %copy-done.2, f32[64,2048]{1,0:T(8,128)} %copy-done.3, ...), custom_call_target="tpu_custom_call" | custom-call | tf_op jit(solution)/shard_map/krylov/pallas_call | solution.py:633
  108.2 11.3 %all_to_all.15.partial = f32[32,1,128]{2,1,0:T(1,128)S(1)} all-to-all(f32[32,1,128]{2,1,0:T(1,128)S(1)} %get-tuple-element.13), channel_id=1, replica_groups=mesh['strip'=32] {'strip'}, dimensions={0} | all-to-all | bytes 32768 | tf_op jit(solution)/shard_map/all_to_all | solution.py:746
  119.5 1.6 %finish.1 = (f32[64,2048]{1,0:T(8,128)}, f32[1,128]{1,0:T(1,128)}) custom-call(f32[32,1,128]{2,1,0:T(1,128)S(1)} %all_to_all.15.partial, f32[4,64,2048]{2,1,0:T(8,128)S(1)} %get-tuple-element.14.basis, f32[16,128]{1,0:T(8,128)S(1)} %bitcast.11), custom_call_target="tpu_custom_call" | custom-call | tf_op jit(solution)/shard_map/finish/pallas_call | solution.py:732
  (12 shorter events, 0.1 us)
Async XLA Ops:
  6.7 56.1 %copy-start = (bf16[512,256]{1,0:T(8,128)(2,1)S(1)}, bf16[512,256]{1,0:T(8,128)(2,1)}, u32[]{:S(2)}) copy-start(bf16[512,256]{1,0:T(8,128)(2,1)} %constant.105.clone.forward_w.inverse_w) | copy-start | bytes 786436
  6.7 56.1 %copy-start.1 = (bf16[512,256]{1,0:T(8,128)(2,1)S(1)}, bf16[512,256]{1,0:T(8,128)(2,1)}, u32[]{:S(2)}) copy-start(bf16[512,256]{1,0:T(8,128)(2,1)} %constant.102.clone.pair_w.inverse_w) | copy-start | bytes 786436
  6.7 56.1 %copy-start.5 = (bf16[512,256]{1,0:T(8,128)(2,1)S(1)}, bf16[512,256]{1,0:T(8,128)(2,1)}, u32[]{:S(2)}) copy-start(bf16[512,256]{1,0:T(8,128)(2,1)} %constant.106.clone.special_f) | copy-start | bytes 786436
  6.7 56.1 %copy-start.6 = (bf16[512,256]{1,0:T(8,128)(2,1)S(1)}, bf16[512,256]{1,0:T(8,128)(2,1)}, u32[]{:S(2)}) copy-start(bf16[512,256]{1,0:T(8,128)(2,1)} %constant.107.clone.special_i) | copy-start | bytes 786436
  6.7 56.1 %copy-start.7 = (f32[128,128]{1,0:T(8,128)S(1)}, f32[128,128]{1,0:T(8,128)}, u32[]{:S(2)}) copy-start(f32[128,128]{1,0:T(8,128)} %constant.104.clone.table) | copy-start | bytes 196612
  6.7 56.1 %all-to-all-start = ((f32[32,128,128]{2,1,0:T(8,128)}), f32[32,128,128]{2,1,0:T(8,128)S(1)}, u32[]{:S(2)}, u32[]{:S(2)}) async-start(f32[32,128,128]{2,1,0:T(8,128)} %row_forward.1), calls=%async_computation | async-start | bytes 4194304 | tf_op jit(solution)/shard_map/all_to_all | solution.py:746
  69.5 4.1 %copy-start.10 = (f32[64,2048]{1,0:T(8,128)S(1)}, f32[64,2048]{1,0:T(8,128)}, u32[]{:S(2)}) copy-start(f32[64,2048]{1,0:T(8,128)} %param.23) | copy-start | bytes 1572868
  69.5 7.6 %copy-start.11 = (s32[2048]{0:T(1024)S(1)}, s32[2048]{0:T(1024)}, u32[]{:S(2)}) copy-start(s32[2048]{0:T(1024)} %param.24) | copy-start | bytes 24580
  69.5 7.6 %copy-start.9 = (f32[2048]{0:T(1024)S(1)}, f32[2048]{0:T(1024)}, u32[]{:S(2)}) copy-start(f32[2048]{0:T(1024)} %param.25) | copy-start | bytes 24580
  69.5 33.5 %all-to-all-start.1 = ((f32[32,1,9344]{2,1,0:T(1,128)}), f32[32,1,9344]{2,1,0:T(1,128)S(1)}, u32[]{:S(2)}, u32[]{:S(2)}) async-start(f32[32,1,9344]{2,1,0:T(1,128)} %bitcast.14), calls=%async_computation.1 | async-start | bytes 2392064 | tf_op jit(solution)/shard_map/all_to_all | solution.py:746
  73.6 8.6 %collective-permute-start = (f32[8,2048]{1,0:T(8,128)S(1)}, f32[8,2048]{1,0:T(8,128)S(1)}, u32[]{:S(2)}, u32[]{:S(2)}) collective-permute-start(f32[8,2048]{1,0:T(8,128)S(1)} %get-tuple-element.17), channel_id=1, source_target_pairs={{0,1},{1,2},{2,3},{3,4},{4,5},{5,6},{6,7},{7,8},{8,9},{9,10},{10,1... | collective-permute-start | bytes 196616 | tf_op jit(solution)/shard_map/ppermute | solution.py:767
  75.8 6.4 %collective-permute-start.1 = (f32[8,2048]{1,0:T(8,128)S(1)}, f32[8,2048]{1,0:T(8,128)S(1)}, u32[]{:S(2)}, u32[]{:S(2)}) collective-permute-start(f32[8,2048]{1,0:T(8,128)S(1)} %get-tuple-element.18), channel_id=1, source_target_pairs={{1,0},{2,1},{3,2},{4,3},{5,4},{6,5},{7,6},{8,7},{9,8},{10,9},{11,1... | collective-permute-start | bytes 196616 | tf_op jit(solution)/shard_map/ppermute | solution.py:768
  77.2 25.8 %copy-start.4 = (bf16[512,256]{1,0:T(8,128)(2,1)S(1)}, bf16[512,256]{1,0:T(8,128)(2,1)}, u32[]{:S(2)}) copy-start(bf16[512,256]{1,0:T(8,128)(2,1)} %constant.108.clone.special_i) | copy-start | bytes 786436
  77.2 25.8 %copy-start.8 = (f32[32,128]{1,0:T(8,128)S(1)}, f32[32,128]{1,0:T(8,128)}, u32[]{:S(2)}) copy-start(f32[32,128]{1,0:T(8,128)} %constant.101.clone.twiddle) | copy-start | bytes 49156
  81.4 0.8 copy-start.2
  82.2 20.8 %copy-start.3 = (f32[64,2048]{1,0:T(8,128)}, f32[64,2048]{1,0:T(8,128)S(1)}, u32[]{:S(2)}) copy-start(f32[64,2048]{1,0:T(8,128)S(1)} %get-tuple-element.11.total_hbm) | copy-start | bytes 1572868

commit v3 on v2

--- a/solution.py
+++ b/solution.py
@@ -201,7 +201,7 @@
 def row_forward(state, noise, step, tables):
     rows, length = state.shape
     factor = length // LANES
-    block = min(32, rows)
+    block = min(64, rows)
     twiddle, pair_w, special_w = tables
     whole = lambda i: (0, 0)
     return pl.pallas_call(
@@ -430,7 +430,7 @@
 def krylov_kernel(
     origin, coefs, source_hbm, count_hbm, total_hbm, twiddle, inverse_w, special_i,
     log_perm_hbm, basis, partial,
-    received, work, kappa, centre, inverse, north, west, east, vector,
+    received, work, kappa, inverse, north, south, west, east, vector,
     source, count, total, log_perm, arrive, leave,
 ):
     inward = [
@@ -544,10 +544,9 @@
         right = here + right
         middle = up + down + left + right
         rest = jnp.where(valid, 1.0 / middle, 0.0)
-        centre[tile] = middle
         inverse[tile] = rest
-        north[tile, :area, :] = up
-        north[tile, area:, :] = rim
+        north[tile] = up
+        south[tile] = down
         west[tile] = left
         east[tile] = right
         first = source[:, lanes]
@@ -561,11 +560,10 @@
         new = vector.at[(step + 1) % 2]
         for tile, here, left, right in sideways(lambda t: now[t, every, :]):
             image = (
-                centre[tile] * here
-                - north[tile, :area, :] * now[tile, before, :]
-                - north[tile, 1 : area + 1, :] * now[tile, after, :]
-                - west[tile] * left
-                - east[tile] * right
+                north[tile] * (here - now[tile, before, :])
+                + south[tile] * (here - now[tile, after, :])
+                + west[tile] * (here - left)
+                + east[tile] * (here - right)
             )
             value = image * inverse[tile]
             new[tile, every, :] = value
@@ -576,6 +574,7 @@
     inward[1].wait()
     inward[2].wait()
     now = vector.at[(ITERS - 1) % 2]
+    first = lax.broadcasted_iota(jnp.int32, (8, LANES), 0) + origin[0] == 0
     back = None
     for tile in range(half):
         lanes = slice(LANES * tile, LANES * (tile + 1))
@@ -583,12 +582,14 @@
         turned = pltpu.roll(here, 1, 1)
         left = jnp.where(first_lane, 0.0 if back is None else back, turned)
         back = turned
-        shared = (
-            north[tile, HALO + 1 : HALO + 1 + rows, :] * now[tile, 9 + HALO : 9 + HALO + rows, :]
-            + west[tile, own, :] * left
-        )
-        energy = here * (centre[tile, own, :] * here - 2.0 * shared)
-        sums[TERMS - 1] = sums[TERMS - 1] + fold_rows(energy)
+        down = here - now[tile, 9 + HALO : 9 + HALO + rows, :]
+        across = here - left
+        energy = fold_rows(south[tile, own, :] * (down * down) + west[tile, own, :] * (across * across))
+        top = here[:8]
+        energy = energy + jnp.where(first, north[tile, HALO : HALO + 8, :] * (top * top), 0.0)
+        if tile == half - 1:
+            energy = energy + fold_rows(jnp.where(last_lane, east[tile, own, :] * (here * here), 0.0))
+        sums[TERMS - 1] = sums[TERMS - 1] + energy
         vectors = [basis[k, :, lanes] for k in range(ITERS)]
         weight = count[:, lanes]
         weighted = [weight * v for v in vectors]
@@ -645,7 +646,7 @@
             padded,
             plane,
             plane,
-            pltpu.VMEM((half, area + 8, LANES), jnp.float32),
+            plane,
             plane,
             plane,
             pltpu.VMEM((2, half, area + 16, LANES), jnp.float32),

time: 122 us -> 121 us (level)
  no operation moved by 1% of the time
where the time goes in v3:
time: 121 us
  waiting for transfers between devices  67.1 us (55%)
  Pallas kernels  22.7 us (19%)
  starting transfers between devices  14.9 us (12%)
  blocking collectives  11.3 us (9%)
  between operations  2.75 us (2%)
    all_to_all x2, waiting for transfers between devices, exchange(): lax.all_to_all(block, 'strip', split_axis=0, concat_axis=0, tiled=True)  67.1 us
    all_to_all x2, starting transfers between devices, exchange(): lax.all_to_all(block, 'strip', split_axis=0, concat_axis=0, tiled=True)  11.4 us
    all_to_all x1, blocking collectives, exchange(): lax.all_to_all(block, 'strip', split_axis=0, concat_axis=0, tiled=True)  11.3 us
    pallas_call x1, Pallas kernels, column_filter(): pl.pallas_call(functools.partial(column_kernel, field_rows=field_rows), i...  6.68 us
    pallas_call x1, Pallas kernels, krylov(): pl.pallas_call(krylov_kernel, in_specs=[pl.BlockSpec(memory_space=pltpu.S...  5.25 us
    pallas_call x1, Pallas kernels, row_forward(): pl.pallas_call(functools.partial(row_kernel, factor=factor), grid=(rows /...  4.97 us
    pallas_call x1, Pallas kernels, observe(): pl.pallas_call(observe_kernel, compiler_params=pltpu.CompilerParams(vmem_...  4.17 us
  transfers between devices with their start and end apart: 4, of which 2 were waited for; matrix products, arithmetic and copies ran while one was open for 1% of the time, Pallas kernels for 3%

profile of v3, /device:TPU:0, one launch (start us, length us, event | category | flops | bytes accessed | tf_op | source)
XLA Modules:
  0.0 120.7 jit_solution(14458196641056986411)
XLA Ops:
  1.3 5.0 %row_forward.1 = f32[32,128,128]{2,1,0:T(8,128)} custom-call(f32[1]{0:T(128)S(6)} %copy.22.step, f32[128,4096]{1,0:T(8,128)} %state.1, f32[128,4096]{1,0:T(8,128)} %noise.1, f32[32,128]{1,0:T(8,128)} %constant.101.clone.twiddle, bf16[512,256]{1,0:T(8,128)(2,1)} %constant.102.clone.pair_w.inverse_w, bf16[512,256]{1,0:T(8,128)(2,1)} %constant.103.clone.special_w), custom_call_target="tpu_custom_call" | custom-call | tf_op jit(solution)/shard_map/row_forward/pallas_call | solution.py:207
  6.3 0.0 copy-start.6
  6.3 0.0 copy-start.7
  6.3 7.3 %all-to-all-start = ((f32[32,128,128]{2,1,0:T(8,128)}), f32[32,128,128]{2,1,0:T(8,128)S(1)}, u32[]{:S(2)}, u32[]{:S(2)}) async-start(f32[32,128,128]{2,1,0:T(8,128)} %row_forward.1), calls=%async_computation | async-start | bytes 4194304 | tf_op jit(solution)/shard_map/all_to_all | solution.py:747
  15.0 0.1 pad_maximum_fusion.1.scale
  15.0 47.3 %all-to-all-done.column = f32[32,128,128]{2,1,0:T(8,128)S(1)} async-done(((f32[32,128,128]{2,1,0:T(8,128)}), f32[32,128,128]{2,1,0:T(8,128)S(1)}, u32[]{:S(2)}, u32[]{:S(2)}) %all-to-all-start) | async-done | bytes 2097184 | tf_op jit(solution)/shard_map/all_to_all | solution.py:747
  62.4 0.0 copy-done
  62.4 0.0 copy-done.1
  62.4 0.0 copy-done.5
  62.4 0.0 copy-done.6
  62.4 0.0 copy-done.7
  62.4 6.7 %column_filter.1 = f32[2336,128]{1,0:T(8,128)} custom-call(f32[2]{0:T(128)S(1)} %pad_maximum_fusion.1.scale, f32[32,128,128]{2,1,0:T(8,128)S(1)} %all-to-all-done.column, f32[128,128]{1,0:T(8,128)S(1)} %copy-done.7, bf16[512,256]{1,0:T(8,128)(2,1)S(1)} %copy-done, bf16[512,256]{1,0:T(8,128)(2,1)S(1)} %copy-done.5, bf16[512,256]{1,0:T(8,128)(2,1)S(1)} %copy-done.1, ...), custom_call_target="tpu_custom_call" | custom-call | tf_op jit(solution)/shard_map/column_filter/pallas_call | solution.py:310
  69.1 4.1 %all-to-all-start.1 = ((f32[32,1,9344]{2,1,0:T(1,128)}), f32[32,1,9344]{2,1,0:T(1,128)S(1)}, u32[]{:S(2)}, u32[]{:S(2)}) async-start(f32[32,1,9344]{2,1,0:T(1,128)} %bitcast.14), calls=%async_computation.1 | async-start | bytes 2392064 | tf_op jit(solution)/shard_map/all_to_all | solution.py:747
  73.2 0.0 copy-done.10
  73.2 2.2 %collective-permute-start = (f32[8,2048]{1,0:T(8,128)S(1)}, f32[8,2048]{1,0:T(8,128)S(1)}, u32[]{:S(2)}, u32[]{:S(2)}) collective-permute-start(f32[8,2048]{1,0:T(8,128)S(1)} %get-tuple-element.17), channel_id=1, source_target_pairs={{0,1},{1,2},{2,3},{3,4},{4,5},{5,6},{6,7},{7,8},{8,9},{9,10},{10,1... | collective-permute-start | bytes 196616 | tf_op jit(solution)/shard_map/ppermute | solution.py:768
  75.4 1.3 %collective-permute-start.1 = (f32[8,2048]{1,0:T(8,128)S(1)}, f32[8,2048]{1,0:T(8,128)S(1)}, u32[]{:S(2)}, u32[]{:S(2)}) collective-permute-start(f32[8,2048]{1,0:T(8,128)S(1)} %get-tuple-element.18), channel_id=1, source_target_pairs={{1,0},{2,1},{3,2},{4,3},{5,4},{6,5},{7,6},{8,7},{9,8},{10,9},{11,1... | collective-permute-start | bytes 196616 | tf_op jit(solution)/shard_map/ppermute | solution.py:769
  76.7 0.0 copy-done.11
  76.7 0.0 copy-done.9
  76.7 0.0 copy-start.4
  76.7 0.0 copy-start.8
  76.7 4.2 %observe.1 = (f32[64,2048]{1,0:T(8,128)S(1)}, f32[64,2048]{1,0:T(8,128)S(1)}) custom-call(s32[1,2048]{1,0:T(1,128)S(1)} %bitcast.13, s32[1,2048]{1,0:T(1,128)S(1)} %bitcast.12, f32[1,2048]{1,0:T(1,128)S(1)} %bitcast.10), custom_call_target="tpu_custom_call" | custom-call | flops 2147483648 | bytes 1048576 | tf_op jit(solution)/shard_map/observe/pallas_call | solution.py:355
  80.9 0.0 copy-start.2
  80.9 0.8 copy-done.2
  81.7 0.1 pad_add_fusion.origin
  81.8 0.0 collective-permute-done
  81.8 0.0 collective-permute-done.1
  81.8 0.9 pad_maximum_fusion.source_hbm
  82.7 19.8 %all-to-all-done.1 = f32[32,1,9344]{2,1,0:T(1,128)S(1)} async-done(((f32[32,1,9344]{2,1,0:T(1,128)}), f32[32,1,9344]{2,1,0:T(1,128)S(1)}, u32[]{:S(2)}, u32[]{:S(2)}) %all-to-all-start.1) | async-done | bytes 1196064 | tf_op jit(solution)/shard_map/all_to_all | solution.py:747
  102.5 0.0 copy-done.4
  102.6 5.2 %krylov.1 = (f32[64,2048]{1,0:T(8,128)}, f32[4,64,2048]{2,1,0:T(8,128)S(1)}, f32[32,1,128]{2,1,0:T(1,128)S(1)}) custom-call(s32[2]{0:T(128)S(1)} %pad_add_fusion.origin, f32[2336,128]{1,0:T(8,128)S(1)} %bitcast.9, f32[80,2048]{1,0:T(8,128)} %pad_maximum_fusion.source_hbm, f32[64,2048]{1,0:T(8,128)} %copy-done.2, f32[64,2048]{1,0:T(8,128)} %copy-done.3, ...), custom_call_target="tpu_custom_call" | custom-call | tf_op jit(solution)/shard_map/krylov/pallas_call | solution.py:634
  107.8 11.3 %all_to_all.15.partial = f32[32,1,128]{2,1,0:T(1,128)S(1)} all-to-all(f32[32,1,128]{2,1,0:T(1,128)S(1)} %get-tuple-element.13), channel_id=1, replica_groups=mesh['strip'=32] {'strip'}, dimensions={0} | all-to-all | bytes 32768 | tf_op jit(solution)/shard_map/all_to_all | solution.py:747
  119.1 1.6 %finish.1 = (f32[64,2048]{1,0:T(8,128)}, f32[1,128]{1,0:T(1,128)}) custom-call(f32[32,1,128]{2,1,0:T(1,128)S(1)} %all_to_all.15.partial, f32[4,64,2048]{2,1,0:T(8,128)S(1)} %get-tuple-element.14.basis, f32[16,128]{1,0:T(8,128)S(1)} %bitcast.11), custom_call_target="tpu_custom_call" | custom-call | tf_op jit(solution)/shard_map/finish/pallas_call | solution.py:733
  (12 shorter events, 0.1 us)
Async XLA Ops:
  6.3 56.1 %copy-start = (bf16[512,256]{1,0:T(8,128)(2,1)S(1)}, bf16[512,256]{1,0:T(8,128)(2,1)}, u32[]{:S(2)}) copy-start(bf16[512,256]{1,0:T(8,128)(2,1)} %constant.105.clone.forward_w.inverse_w) | copy-start | bytes 786436
  6.3 56.1 %copy-start.1 = (bf16[512,256]{1,0:T(8,128)(2,1)S(1)}, bf16[512,256]{1,0:T(8,128)(2,1)}, u32[]{:S(2)}) copy-start(bf16[512,256]{1,0:T(8,128)(2,1)} %constant.102.clone.pair_w.inverse_w) | copy-start | bytes 786436
  6.3 56.1 %copy-start.5 = (bf16[512,256]{1,0:T(8,128)(2,1)S(1)}, bf16[512,256]{1,0:T(8,128)(2,1)}, u32[]{:S(2)}) copy-start(bf16[512,256]{1,0:T(8,128)(2,1)} %constant.106.clone.special_f) | copy-start | bytes 786436
  6.3 56.1 %copy-start.6 = (bf16[512,256]{1,0:T(8,128)(2,1)S(1)}, bf16[512,256]{1,0:T(8,128)(2,1)}, u32[]{:S(2)}) copy-start(bf16[512,256]{1,0:T(8,128)(2,1)} %constant.107.clone.special_i) | copy-start | bytes 786436
  6.3 56.1 %copy-start.7 = (f32[128,128]{1,0:T(8,128)S(1)}, f32[128,128]{1,0:T(8,128)}, u32[]{:S(2)}) copy-start(f32[128,128]{1,0:T(8,128)} %constant.104.clone.table) | copy-start | bytes 196612
  6.3 56.1 %all-to-all-start = ((f32[32,128,128]{2,1,0:T(8,128)}), f32[32,128,128]{2,1,0:T(8,128)S(1)}, u32[]{:S(2)}, u32[]{:S(2)}) async-start(f32[32,128,128]{2,1,0:T(8,128)} %row_forward.1), calls=%async_computation | async-start | bytes 4194304 | tf_op jit(solution)/shard_map/all_to_all | solution.py:747
  69.1 4.1 %copy-start.10 = (f32[64,2048]{1,0:T(8,128)S(1)}, f32[64,2048]{1,0:T(8,128)}, u32[]{:S(2)}) copy-start(f32[64,2048]{1,0:T(8,128)} %param.23) | copy-start | bytes 1572868
  69.1 7.6 %copy-start.11 = (s32[2048]{0:T(1024)S(1)}, s32[2048]{0:T(1024)}, u32[]{:S(2)}) copy-start(s32[2048]{0:T(1024)} %param.24) | copy-start | bytes 24580
  69.1 7.6 %copy-start.9 = (f32[2048]{0:T(1024)S(1)}, f32[2048]{0:T(1024)}, u32[]{:S(2)}) copy-start(f32[2048]{0:T(1024)} %param.25) | copy-start | bytes 24580
  69.1 33.5 %all-to-all-start.1 = ((f32[32,1,9344]{2,1,0:T(1,128)}), f32[32,1,9344]{2,1,0:T(1,128)S(1)}, u32[]{:S(2)}, u32[]{:S(2)}) async-start(f32[32,1,9344]{2,1,0:T(1,128)} %bitcast.14), calls=%async_computation.1 | async-start | bytes 2392064 | tf_op jit(solution)/shard_map/all_to_all | solution.py:747
  73.2 8.6 %collective-permute-start = (f32[8,2048]{1,0:T(8,128)S(1)}, f32[8,2048]{1,0:T(8,128)S(1)}, u32[]{:S(2)}, u32[]{:S(2)}) collective-permute-start(f32[8,2048]{1,0:T(8,128)S(1)} %get-tuple-element.17), channel_id=1, source_target_pairs={{0,1},{1,2},{2,3},{3,4},{4,5},{5,6},{6,7},{7,8},{8,9},{9,10},{10,1... | collective-permute-start | bytes 196616 | tf_op jit(solution)/shard_map/ppermute | solution.py:768
  75.4 6.4 %collective-permute-start.1 = (f32[8,2048]{1,0:T(8,128)S(1)}, f32[8,2048]{1,0:T(8,128)S(1)}, u32[]{:S(2)}, u32[]{:S(2)}) collective-permute-start(f32[8,2048]{1,0:T(8,128)S(1)} %get-tuple-element.18), channel_id=1, source_target_pairs={{1,0},{2,1},{3,2},{4,3},{5,4},{6,5},{7,6},{8,7},{9,8},{10,9},{11,1... | collective-permute-start | bytes 196616 | tf_op jit(solution)/shard_map/ppermute | solution.py:769
  76.7 25.8 %copy-start.4 = (bf16[512,256]{1,0:T(8,128)(2,1)S(1)}, bf16[512,256]{1,0:T(8,128)(2,1)}, u32[]{:S(2)}) copy-start(bf16[512,256]{1,0:T(8,128)(2,1)} %constant.108.clone.special_i) | copy-start | bytes 786436
  76.7 25.8 %copy-start.8 = (f32[32,128]{1,0:T(8,128)S(1)}, f32[32,128]{1,0:T(8,128)}, u32[]{:S(2)}) copy-start(f32[32,128]{1,0:T(8,128)} %constant.101.clone.twiddle) | copy-start | bytes 49156
  80.9 0.8 copy-start.2
  81.7 20.8 %copy-start.3 = (f32[64,2048]{1,0:T(8,128)}, f32[64,2048]{1,0:T(8,128)S(1)}, u32[]{:S(2)}) copy-start(f32[64,2048]{1,0:T(8,128)S(1)} %get-tuple-element.11.total_hbm) | copy-start | bytes 1572868

commit v4 on v3

--- a/solution.py
+++ b/solution.py
@@ -8,6 +8,7 @@
 from jax.experimental import pallas as pl
 from jax.experimental.pallas import tpu as pltpu
 from jax.sharding import PartitionSpec as P
+
 
 ITERS = 4
 LANES = 128
@@ -224,7 +225,8 @@
 
 
 def column_kernel(
-    scale, column, table, forward_w, special_f, inverse_w, special_i, wave, out, work, field, *, field_rows
+    origin, scale, column, table, forward_w, special_f, inverse_w, special_i, wave, count, total,
+    out, work, field, *, field_rows,
 ):
     factor, _, width = column.shape
     half = factor // 2
@@ -303,22 +305,24 @@
         out[extent * part : extent * (part + 1), :] = field[begin : begin + extent, :]
 
 
-def column_filter(column, scale, wave, tables, parts, field_rows):
+def column_filter(column, scale, wave, tables, parts, field_rows, ready):
     factor, _, width = column.shape
     length = factor * LANES
     vmem = pl.BlockSpec(memory_space=pltpu.VMEM)
     return pl.pallas_call(
         functools.partial(column_kernel, field_rows=field_rows),
-        in_specs=[pl.BlockSpec(memory_space=pltpu.SMEM)] + [vmem] * 7,
+        in_specs=[pl.BlockSpec(memory_space=pltpu.SMEM)] * 2
+        + [vmem] * 7
+        + [pl.BlockSpec(memory_space=pl.ANY)] * 2,
         out_specs=vmem,
-        out_shape=pltpu.HBM((parts * (field_rows + ABOVE + BELOW), width), jnp.float32),
+        out_shape=pltpu.VMEM((parts * (field_rows + ABOVE + BELOW), width), jnp.float32),
         scratch_shapes=[
             pltpu.VMEM((factor // 2, 2 * LANES, width), jnp.float32),
             pltpu.VMEM((length // 2 + 2 * HALO, width), jnp.float32),
         ],
         compiler_params=pltpu.CompilerParams(vmem_limit_bytes=24 << 20),
         name="column_filter",
-    )(scale, near(column), *tables, wave)
+    )(ready[0], scale, near(column), *tables, wave, *(far(value) for value in ready[1:]))
 
 
 def observe_kernel(local, cells, values, count, total, left):
@@ -428,7 +432,7 @@
 
 
 def krylov_kernel(
-    origin, coefs, source_hbm, count_hbm, total_hbm, twiddle, inverse_w, special_i,
+    origin, coefs, above, middle, below, count_hbm, total_hbm, twiddle, inverse_w, special_i,
     log_perm_hbm, basis, partial,
     received, work, kappa, inverse, north, south, west, east, vector,
     source, count, total, log_perm, arrive, leave,
@@ -436,7 +440,13 @@
     inward = [
         pltpu.make_async_copy(far_ref, near_ref, arrive.at[k])
         for k, (far_ref, near_ref) in enumerate(
-            ((source_hbm, source), (count_hbm, count), (total_hbm, total))
+            (
+                (above, source.at[:HALO, :]),
+                (middle, source.at[HALO : HALO + middle.shape[0], :]),
+                (below, source.at[HALO + middle.shape[0] :, :]),
+                (count_hbm, count),
+                (total_hbm, total),
+            )
         )
     ]
     outward = pltpu.make_async_copy(log_perm, log_perm_hbm, leave)
@@ -508,7 +518,8 @@
 
     lax.fori_loop(0, groups, inverse_group, 0, unroll=2)
     outward.start()
-    inward[0].wait()
+    for copy in inward[:3]:
+        copy.wait()
 
     first_lane = lax.broadcasted_iota(jnp.int32, (1, LANES), 1) == 0
     last_lane = lax.broadcasted_iota(jnp.int32, (1, LANES), 1) == LANES - 1
@@ -542,8 +553,7 @@
         down = here + kappa[tile, after, :]
         left = here + left
         right = here + right
-        middle = up + down + left + right
-        rest = jnp.where(valid, 1.0 / middle, 0.0)
+        rest = jnp.where(valid, 1.0 / (up + down + left + right), 0.0)
         inverse[tile] = rest
         north[tile] = up
         south[tile] = down
@@ -571,8 +581,8 @@
             sums[2 * step + 1] = sums[2 * step + 1] + fold_rows((here * image)[own])
             sums[2 * step + 2] = sums[2 * step + 2] + fold_rows((value * image)[own])
 
-    inward[1].wait()
-    inward[2].wait()
+    inward[3].wait()
+    inward[4].wait()
     now = vector.at[(ITERS - 1) % 2]
     first = lax.broadcasted_iota(jnp.int32, (8, LANES), 0) + origin[0] == 0
     back = None
@@ -622,10 +632,10 @@
     outward.wait()
 
 
-def krylov(origin, coefs, source, count, total, tables, parts):
-    area, columns = source.shape
+def krylov(origin, coefs, pieces_of_source, count, total, tables, parts):
+    rows, columns = count.shape
     half = columns // LANES
-    rows = area - 2 * HALO
+    area = rows + 2 * HALO
     vmem = pl.BlockSpec(memory_space=pltpu.VMEM)
     anywhere = pl.BlockSpec(memory_space=pl.ANY)
     plane = pltpu.VMEM((half, area, LANES), jnp.float32)
@@ -633,7 +643,7 @@
     strip = pltpu.VMEM((rows, columns), jnp.float32)
     return pl.pallas_call(
         krylov_kernel,
-        in_specs=[pl.BlockSpec(memory_space=pltpu.SMEM), vmem] + [anywhere] * 3 + [vmem] * 3,
+        in_specs=[pl.BlockSpec(memory_space=pltpu.SMEM), vmem] + [anywhere] * 5 + [vmem] * 3,
         out_specs=(anywhere, vmem, vmem),
         out_shape=(
             pltpu.HBM((rows, columns), jnp.float32),
@@ -654,12 +664,12 @@
             strip,
             strip,
             strip,
-            pltpu.SemaphoreType.DMA((3,)),
+            pltpu.SemaphoreType.DMA((5,)),
             pltpu.SemaphoreType.DMA(()),
         ],
         compiler_params=pltpu.CompilerParams(vmem_limit_bytes=32 << 20),
         name="krylov",
-    )(origin, near(coefs), far(source), far(count), far(total), *tables)
+    )(origin, near(coefs), *(far(v) for v in (*pieces_of_source, count, total)), *tables)
 
 
 def final_kernel(partial, basis, values, pressure, loglik):
@@ -747,7 +757,7 @@
     return lax.all_to_all(block, "strip", split_axis=0, concat_axis=0, tiled=True)
 
 
-def body(state, noise, step, field_scale, wave_scale, source, obs_cells, obs_values):
+def steps(state, noise, step, field_scale, wave_scale, source, obs_cells, obs_values):
     parts = lax.axis_size("strip")
     position = lax.axis_index("strip")
     rows_here, length = state.shape
@@ -767,12 +777,13 @@
     behind = [(b, a) for a, b in ahead]
     above = lax.ppermute(source[field_rows - HALO :], "strip", ahead)
     below = lax.ppermute(source[:HALO], "strip", behind)
-    wide_source = jnp.concatenate([above, source, below], axis=0)
 
     cell_row = obs_cells // columns - position * field_rows
     count, total = observe(
         cell_row[None, :], (obs_cells % columns)[None, :], obs_values[None, :], field_rows, columns
     )
+
+    origin = jnp.stack([position * field_rows, parts * field_rows]).astype(jnp.int32)
 
     tiles = row_forward(state, noise, step, (across, pieces(forward), pieces(special_f)))
     if ways > 1:
@@ -803,16 +814,17 @@
         (down, *(pieces(t.T) for t in (forward, special_f, inverse, special_i))),
         parts,
         field_rows,
+        (origin, count, total),
     )
+    blocks, above, below = lax.optimization_barrier((blocks, above, below))
     extent = field_rows + ABOVE + BELOW
     coefs = exchange(blocks.reshape(parts, 1, extent * width))
     if ways > 1:
         coefs = coefs.reshape(factor, ways, extent, width).transpose(0, 2, 1, 3)
     coefs = coefs.reshape(factor * extent, LANES)
 
-    origin = jnp.stack([position * field_rows, parts * field_rows]).astype(jnp.int32)
     log_perm, basis, partial = krylov(
-        origin, coefs, wide_source, count, total, (across, pieces(inverse), pieces(special_i)), parts
+        origin, coefs, (above, source, below), count, total, (across, pieces(inverse), pieces(special_i)), parts
     )
     pressure, loglik = finish(exchange(partial), basis, obs_values.reshape(-1, LANES))
     return (log_perm, pressure, loglik[0, 0])
@@ -821,7 +833,7 @@
 def solution(mesh):
     placed = (P("strip", None), P("strip", None), P(), P(), P(), P("strip", None), P(), P())
     return jax.shard_map(
-        body,
+        steps,
         mesh=mesh,
         in_specs=placed,
         out_specs=(P("strip", None), P("strip", None), P()),

time: 121 us -> 120 us (level)
  blocking collectives: 11.3 us -> 43.9 us
  waiting for transfers between devices: 67.1 us -> 37 us
  starting transfers between devices: 14.9 us -> 10.8 us
  local copies, waits for them, and re-layouts: 0.85 us -> 2.52 us
    all_to_all x1 -> x2, blocking collectives: 11.3 us -> 43.9 us  [exchange(): lax.all_to_all(block, 'strip', split_axis=0, concat_axis=0, tiled=True)]
    all_to_all x2 -> x1, waiting for transfers between devices: 67.1 us -> 37 us  [exchange(): lax.all_to_all(block, 'strip', split_axis=0, concat_axis=0, tiled=True)]
    all_to_all x2 -> x1, starting transfers between devices: 11.4 us -> 7.32 us  [exchange(): lax.all_to_all(block, 'strip', split_axis=0, concat_axis=0, tiled=True)]
  transfers between devices with their start and end apart: 4 -> 3, of which waited for: 2 -> 1; matrix products, arithmetic and copies ran while one was open for 1% -> 1% of each run, Pallas kernels for 3% -> 8%
where the time goes in v4:
time: 120 us; the launch traced here: 119 us
  blocking collectives  43.9 us (37%)
  waiting for transfers between devices  37 us (31%)
  Pallas kernels  22.1 us (18%)
  starting transfers between devices  10.8 us (9%)
  between operations  2.78 us (2%)
  local copies, waits for them, and re-layouts  2.52 us (2%)
    all_to_all x2, blocking collectives, exchange(): lax.all_to_all(block, 'strip', split_axis=0, concat_axis=0, tiled=True)  43.9 us
    all_to_all x1, waiting for transfers between devices, exchange(): lax.all_to_all(block, 'strip', split_axis=0, concat_axis=0, tiled=True)  37 us
    all_to_all x1, starting transfers between devices, exchange(): lax.all_to_all(block, 'strip', split_axis=0, concat_axis=0, tiled=True)  7.32 us
    pallas_call x1, Pallas kernels, krylov(): pl.pallas_call(krylov_kernel, in_specs=[pl.BlockSpec(memory_space=pltpu.S...  5.75 us
    pallas_call x1, Pallas kernels, column_filter(): pl.pallas_call(functools.partial(column_kernel, field_rows=field_rows), i...  5.68 us
    pallas_call x1, Pallas kernels, row_forward(): pl.pallas_call(functools.partial(row_kernel, factor=factor), grid=(rows /...  4.92 us
    pallas_call x1, Pallas kernels, observe(): pl.pallas_call(observe_kernel, compiler_params=pltpu.CompilerParams(vmem_...  4.18 us
  transfers between devices with their start and end apart: 3, of which 1 were waited for; matrix products, arithmetic and copies ran while one was open for 1% of the time, Pallas kernels for 8%

profile of v4, /device:TPU:0, one launch (start us, length us, event | category | flops | bytes accessed | tf_op | source)
XLA Modules:
  0.0 119.4 jit_solution(9132291199385661840)
XLA Ops:
  1.3 4.9 %row_forward.1 = f32[32,128,128]{2,1,0:T(8,128)} custom-call(f32[1]{0:T(128)S(6)} %copy.22.step, f32[128,4096]{1,0:T(8,128)} %state.1, f32[128,4096]{1,0:T(8,128)} %noise.1, f32[32,128]{1,0:T(8,128)} %constant.101.clone.twiddle, bf16[512,256]{1,0:T(8,128)(2,1)} %constant.102.clone.pair_w.inverse_w, bf16[512,256]{1,0:T(8,128)(2,1)} %constant.103.clone.special_w), custom_call_target="tpu_custom_call" | custom-call | tf_op jit(solution)/shard_map/row_forward/pallas_call | solution.py:208
  6.2 7.3 %all-to-all-start = ((f32[32,128,128]{2,1,0:T(8,128)}), f32[32,128,128]{2,1,0:T(8,128)S(1)}, u32[]{:S(2)}, u32[]{:S(2)}) async-start(f32[32,128,128]{2,1,0:T(8,128)} %row_forward.1), calls=%async_computation | async-start | bytes 4194304 | tf_op jit(solution)/shard_map/all_to_all | solution.py:757
  13.5 0.9 fusion.8
  14.4 2.2 %collective-permute-start = (f32[8,2048]{1,0:T(8,128)S(1)}, f32[8,2048]{1,0:T(8,128)S(1)}, u32[]{:S(2)}, u32[]{:S(2)}) collective-permute-start(f32[8,2048]{1,0:T(8,128)S(1)} %get-tuple-element.24), channel_id=1, source_target_pairs={{0,1},{1,2},{2,3},{3,4},{4,5},{5,6},{6,7},{7,8},{8,9},{9,10},{10,1... | collective-permute-start | bytes 196616 | tf_op jit(solution)/shard_map/ppermute | solution.py:778
  16.6 1.3 %collective-permute-start.1 = (f32[8,2048]{1,0:T(8,128)S(1)}, f32[8,2048]{1,0:T(8,128)S(1)}, u32[]{:S(2)}, u32[]{:S(2)}) collective-permute-start(f32[8,2048]{1,0:T(8,128)S(1)} %get-tuple-element.23), channel_id=1, source_target_pairs={{1,0},{2,1},{3,2},{4,3},{5,4},{6,5},{7,6},{8,7},{9,8},{10,9},{11,1... | collective-permute-start | bytes 196616 | tf_op jit(solution)/shard_map/ppermute | solution.py:779
  19.2 0.1 pad_add_fusion.origin
  19.3 0.0 copy-done.12
  19.3 0.0 copy-done.9
  19.3 0.0 copy-start.2
  19.3 0.0 copy-start.3
  19.3 0.0 copy-start.5
  19.4 0.0 copy-start.6
  19.4 0.0 copy-start.7
  19.4 4.2 %observe.1 = (f32[64,2048]{1,0:T(8,128)S(1)}, f32[64,2048]{1,0:T(8,128)S(1)}) custom-call(s32[1,2048]{1,0:T(1,128)S(1)} %bitcast.14, s32[1,2048]{1,0:T(1,128)S(1)} %bitcast.13, f32[1,2048]{1,0:T(1,128)S(1)} %bitcast.11), custom_call_target="tpu_custom_call" | custom-call | flops 2147483648 | bytes 1048576 | tf_op jit(solution)/shard_map/observe/pallas_call | solution.py:359
  23.6 0.0 copy-start
  23.6 0.8 copy-done
  24.4 0.8 copy-done.1
  25.2 0.1 pad_maximum_fusion.scale
  25.2 37.0 %all-to-all-done.column = f32[32,128,128]{2,1,0:T(8,128)S(1)} async-done(((f32[32,128,128]{2,1,0:T(8,128)}), f32[32,128,128]{2,1,0:T(8,128)S(1)}, u32[]{:S(2)}, u32[]{:S(2)}) %all-to-all-start) | async-done | bytes 2097184 | tf_op jit(solution)/shard_map/all_to_all | solution.py:757
  62.3 0.0 copy-done.2
  62.3 0.0 copy-done.3
  62.3 5.7 %column_filter.1 = f32[2336,128]{1,0:T(8,128)S(1)} custom-call(s32[2]{0:T(128)S(1)} %pad_add_fusion.origin, f32[2]{0:T(128)S(1)} %pad_maximum_fusion.scale, f32[32,128,128]{2,1,0:T(8,128)S(1)} %all-to-all-done.column, f32[128,128]{1,0:T(8,128)S(1)} %copy-done.7, bf16[512,256]{1,0:T(8,128)(2,1)S(1)} %copy-done.2, bf16[512,256]{1,0:T(8,128)(2,1)S(1)} %copy-done.5, ...), custom_call_target="tpu_custom_call" | custom-call | tf_op jit(solution)/shard_map/column_filter/pallas_call | solution.py:312
  68.0 0.0 copy-start.4
  68.0 0.0 copy-start.8
  68.0 0.0 collective-permute-done.above
  68.0 0.0 collective-permute-done.1.below
  68.0 0.0 copy-start.11
  68.0 34.9 %all_to_all.15 = f32[32,1,9344]{2,1,0:T(1,128)S(1)} all-to-all(f32[32,1,9344]{2,1,0:T(1,128)S(1)} %bitcast.9), channel_id=1, replica_groups=mesh['strip'=32] {'strip'}, dimensions={0} | all-to-all | bytes 2392064 | tf_op jit(solution)/shard_map/all_to_all | solution.py:757
  103.0 0.0 copy-done.11
  103.0 5.7 %krylov.1 = (f32[64,2048]{1,0:T(8,128)}, f32[4,64,2048]{2,1,0:T(8,128)S(1)}, f32[32,1,128]{2,1,0:T(1,128)S(1)}) custom-call(s32[2]{0:T(128)S(1)} %pad_add_fusion.origin, f32[2336,128]{1,0:T(8,128)S(1)} %bitcast.10, f32[8,2048]{1,0:T(8,128)} %copy-done.10, f32[64,2048]{1,0:T(8,128)} %middle.1, f32[8,2048]{1,0:T(8,128)} %copy-done.11, f32[64,2048]{1,0:T(8,128)} %copy-done, ...), custom_call_target="tpu_custom_call" | custom-call | tf_op jit(solution)/shard_map/krylov/pallas_call | solution.py:644
  108.7 9.0 %all_to_all.16.partial = f32[32,1,128]{2,1,0:T(1,128)S(1)} all-to-all(f32[32,1,128]{2,1,0:T(1,128)S(1)} %get-tuple-element.19), channel_id=1, replica_groups=mesh['strip'=32] {'strip'}, dimensions={0} | all-to-all | bytes 32768 | tf_op jit(solution)/shard_map/all_to_all | solution.py:757
  117.7 1.6 %finish.1 = (f32[64,2048]{1,0:T(8,128)}, f32[1,128]{1,0:T(1,128)}) custom-call(f32[32,1,128]{2,1,0:T(1,128)S(1)} %all_to_all.16.partial, f32[4,64,2048]{2,1,0:T(8,128)S(1)} %get-tuple-element.20.basis, f32[16,128]{1,0:T(8,128)S(1)} %bitcast.12), custom_call_target="tpu_custom_call" | custom-call | tf_op jit(solution)/shard_map/finish/pallas_call | solution.py:743
  (12 shorter events, 0.1 us)
Async XLA Ops:
  6.2 13.1 %copy-start.12 = (s32[2048]{0:T(1024)S(1)}, s32[2048]{0:T(1024)}, u32[]{:S(2)}) copy-start(s32[2048]{0:T(1024)} %param.24) | copy-start | bytes 24580
  6.2 13.1 %copy-start.9 = (f32[2048]{0:T(1024)S(1)}, f32[2048]{0:T(1024)}, u32[]{:S(2)}) copy-start(f32[2048]{0:T(1024)} %param.25) | copy-start | bytes 24580
  6.2 56.1 %all-to-all-start = ((f32[32,128,128]{2,1,0:T(8,128)}), f32[32,128,128]{2,1,0:T(8,128)S(1)}, u32[]{:S(2)}, u32[]{:S(2)}) async-start(f32[32,128,128]{2,1,0:T(8,128)} %row_forward.1), calls=%async_computation | async-start | bytes 4194304 | tf_op jit(solution)/shard_map/all_to_all | solution.py:757
  14.4 53.6 %collective-permute-start = (f32[8,2048]{1,0:T(8,128)S(1)}, f32[8,2048]{1,0:T(8,128)S(1)}, u32[]{:S(2)}, u32[]{:S(2)}) collective-permute-start(f32[8,2048]{1,0:T(8,128)S(1)} %get-tuple-element.24), channel_id=1, source_target_pairs={{0,1},{1,2},{2,3},{3,4},{4,5},{5,6},{6,7},{7,8},{8,9},{9,10},{10,1... | collective-permute-start | bytes 196616 | tf_op jit(solution)/shard_map/ppermute | solution.py:778
  16.6 51.4 %collective-permute-start.1 = (f32[8,2048]{1,0:T(8,128)S(1)}, f32[8,2048]{1,0:T(8,128)S(1)}, u32[]{:S(2)}, u32[]{:S(2)}) collective-permute-start(f32[8,2048]{1,0:T(8,128)S(1)} %get-tuple-element.23), channel_id=1, source_target_pairs={{1,0},{2,1},{3,2},{4,3},{5,4},{6,5},{7,6},{8,7},{9,8},{10,9},{11,1... | collective-permute-start | bytes 196616 | tf_op jit(solution)/shard_map/ppermute | solution.py:779
  19.3 42.9 %copy-start.2 = (bf16[512,256]{1,0:T(8,128)(2,1)S(1)}, bf16[512,256]{1,0:T(8,128)(2,1)}, u32[]{:S(2)}) copy-start(bf16[512,256]{1,0:T(8,128)(2,1)} %constant.105.clone.forward_w.inverse_w) | copy-start | bytes 786436
  19.3 42.9 %copy-start.3 = (bf16[512,256]{1,0:T(8,128)(2,1)S(1)}, bf16[512,256]{1,0:T(8,128)(2,1)}, u32[]{:S(2)}) copy-start(bf16[512,256]{1,0:T(8,128)(2,1)} %constant.102.clone.pair_w.inverse_w) | copy-start | bytes 786436
  19.3 42.9 %copy-start.5 = (bf16[512,256]{1,0:T(8,128)(2,1)S(1)}, bf16[512,256]{1,0:T(8,128)(2,1)}, u32[]{:S(2)}) copy-start(bf16[512,256]{1,0:T(8,128)(2,1)} %constant.106.clone.special_f) | copy-start | bytes 786436
  19.4 42.9 %copy-start.6 = (bf16[512,256]{1,0:T(8,128)(2,1)S(1)}, bf16[512,256]{1,0:T(8,128)(2,1)}, u32[]{:S(2)}) copy-start(bf16[512,256]{1,0:T(8,128)(2,1)} %constant.107.clone.special_i) | copy-start | bytes 786436
  19.4 42.9 %copy-start.7 = (f32[128,128]{1,0:T(8,128)S(1)}, f32[128,128]{1,0:T(8,128)}, u32[]{:S(2)}) copy-start(f32[128,128]{1,0:T(8,128)} %constant.104.clone.table) | copy-start | bytes 196612
  23.6 0.8 copy-start
  24.4 0.8 copy-start.1
  68.0 35.0 %copy-start.4 = (bf16[512,256]{1,0:T(8,128)(2,1)S(1)}, bf16[512,256]{1,0:T(8,128)(2,1)}, u32[]{:S(2)}) copy-start(bf16[512,256]{1,0:T(8,128)(2,1)} %constant.108.clone.special_i) | copy-start | bytes 786436
  68.0 35.0 %copy-start.8 = (f32[32,128]{1,0:T(8,128)S(1)}, f32[32,128]{1,0:T(8,128)}, u32[]{:S(2)}) copy-start(f32[32,128]{1,0:T(8,128)} %constant.101.clone.twiddle) | copy-start | bytes 49156
  68.0 34.9 %copy-start.10 = (f32[8,2048]{1,0:T(8,128)}, f32[8,2048]{1,0:T(8,128)S(1)}, u32[]{:S(2)}) copy-start(f32[8,2048]{1,0:T(8,128)S(1)} %collective-permute-done.above) | copy-start | bytes 196612
  68.0 34.9 %copy-start.11 = (f32[8,2048]{1,0:T(8,128)}, f32[8,2048]{1,0:T(8,128)S(1)}, u32[]{:S(2)}) copy-start(f32[8,2048]{1,0:T(8,128)S(1)} %collective-permute-done.1.below) | copy-start | bytes 196612
